TPU v7x, 128 devices: a whole 4x4x4 slice. The times are simulated.
128 devices in a mesh: gz: 2 (over x_lo), gx: 2 (over core), gy: 32 (over z, y, x_hi).
Axes of the slice: x: 4 (x_hi: 2, x_lo: 2; x = x_hi * 2 + x_lo), y: 4, z: 4, core: 2. Of those that a mesh axis runs over, the one named last changes fastest.
Arguments:
- initial_field: float32 [128, 16, 4096], P('gz', 'gx', 'gy'), may hold values from -36 to 36
- plane_coupling: float32 [128, 16, 4096], P('gz', 'gx', 'gy'), may hold values from 0.06 to 0.24
- line_coupling: float32 [128, 16, 4096], P('gz', 'gx', 'gy'), may hold values from 1000 to 8000
- source: float32 [128, 16, 4096], P('gz', 'gx', 'gy'), may hold values from -4 to 4, as said below
- shift_table: float32 [8], replicated, may hold values from 0.5 to 1
- shift_index: int32 [4], replicated, may hold values from 0 to 7
Outputs:
- heated: float32 [128, 16, 4096], P('gz', 'gx', 'gy')
Inputs may be any that keep to these rules, and one draw needn't show every extreme that they name: `shift_index`: one table row for each half-step. A heat source.
All inputs are finite; a program needn't handle non-finite values.
Results may differ from a plain program's by a relative error of at most 0.0003.
Values sent between devices are 32-bit elements; how exact they have to be, the bound alone decides.
A program may use at most 64 MiB of HBM per device.

v0:
```python
import jax
import jax.numpy as jnp
from jax import lax
from jax.sharding import PartitionSpec as P

HALF = 4


def joined_along(parts, dim):
    shape = list(parts.shape[1:])
    shape[dim] *= parts.shape[0]
    return jnp.moveaxis(parts, 0, dim).reshape(shape)


def copy_for_each(x, axis):
    copies = jnp.broadcast_to(x, (lax.axis_size(axis), *x.shape))
    return lax.all_to_all(copies, axis, split_axis=0, concat_axis=0, tiled=True)


def gathered_copies(x, axis, dim):
    return joined_along(copy_for_each(x, axis), dim)


def side_by_side(arrays, axis, dim, along):
    ends, at = ([], 0)
    for a in arrays[:-1]:
        at += a.shape[along]
        ends.append(at)
    both = jnp.concatenate(arrays, axis=along)
    return tuple(jnp.split(gathered_copies(both, axis, dim), ends, axis=along))


def padded_2(x, sides, width):
    edges = {}
    for axis, dim in sides:
        size, length = (lax.axis_size(axis), x.shape[dim])
        up = [(i, (i + 1) % size) for i in range(size - 1)]
        last = lax.slice_in_dim(x, length - width, length, axis=dim)
        first = lax.slice_in_dim(x, 0, width, axis=dim)
        edges[dim] = (
            lax.ppermute(last, axis, up),
            lax.ppermute(first, axis, [(b, a) for a, b in up]),
        )
    done = []
    for _, dim in sides:
        low, high = edges[dim]
        around = [(width, width) if d in done else (0, 0) for d in range(x.ndim)]
        x = jnp.concatenate([jnp.pad(low, around), x, jnp.pad(high, around)], axis=dim)
        done.append(dim)
    return x


def lookup(shift_table, table_row):
    table_slots = jnp.arange(shift_table.shape[0], dtype=jnp.int32)
    return jnp.sum(jnp.where(table_slots == table_row, shift_table, jnp.zeros_like(shift_table)))


def from_below(values, stride, fill_value, which_axis):
    filler_shape = list(values.shape)
    filler_shape[which_axis] = stride
    filler = jnp.full(filler_shape, fill_value, values.dtype)
    retained = lax.slice_in_dim(values, 0, values.shape[which_axis] - stride, axis=which_axis)
    return jnp.concatenate([filler, retained], axis=which_axis)


def from_above(values, stride, fill_value, which_axis):
    filler_shape = list(values.shape)
    filler_shape[which_axis] = stride
    filler = jnp.full(filler_shape, fill_value, values.dtype)
    retained = lax.slice_in_dim(values, stride, values.shape[which_axis], axis=which_axis)
    return jnp.concatenate([retained, filler], axis=which_axis)


def local_solve(scaled, forcing):
    lower_band = -scaled
    upper_band = -scaled
    main_band = 1.0 + 2.0 * scaled
    layer_count = scaled.shape[0]
    stride = 1
    while stride < layer_count:
        lower_before = from_below(lower_band, stride, 0.0, 0)
        main_before = from_below(main_band, stride, 1.0, 0)
        upper_before = from_below(upper_band, stride, 0.0, 0)
        forcing_before = from_below(forcing, stride, 0.0, 1)
        lower_after = from_above(lower_band, stride, 0.0, 0)
        main_after = from_above(main_band, stride, 1.0, 0)
        upper_after = from_above(upper_band, stride, 0.0, 0)
        forcing_after = from_above(forcing, stride, 0.0, 1)
        left_factor = -lower_band / main_before
        right_factor = -upper_band / main_after
        main_band = main_band + left_factor * upper_before + right_factor * lower_after
        forcing = forcing + left_factor * forcing_before + right_factor * forcing_after
        lower_band = left_factor * lower_before
        upper_band = right_factor * upper_after
        stride = stride * 2
    return forcing / main_band


def reduced_gathered(first_y, last_y, first_f, last_f, first_g, last_g):
    gathered = side_by_side(
        (first_y[None], last_y[None], first_f[None], last_f[None], first_g[None], last_g[None]),
        "gz",
        0,
        1,
    )
    zero_plane = jnp.zeros_like(first_y)

    def forward(previous, entries):
        offset, slope_part = previous
        start_y, end_y, start_f, end_f, start_g, end_g = entries
        pivot_value = 1.0 - start_f * slope_part
        constant = (start_y + start_f * offset) / pivot_value
        factor = start_g / pivot_value
        next_offset = end_y + end_f * (offset + slope_part * start_y) / pivot_value
        next_slope = end_g + end_f * slope_part * start_g / pivot_value
        return ((next_offset, next_slope), (offset, slope_part, constant, factor))

    final_state, outcome = lax.scan(forward, (zero_plane, zero_plane), gathered)
    offsets, slopes, constants, factors = outcome

    def backward(later_value, entries):
        constant, factor = entries
        own_value = constant + factor * later_value
        return (own_value, (own_value, later_value))

    final_value, solved = lax.scan(backward, zero_plane, (constants, factors), reverse=True)
    own_values, next_values = solved
    device = lax.axis_index("gz")
    offset = lax.dynamic_index_in_dim(offsets, device, 0, keepdims=False)
    slope_part = lax.dynamic_index_in_dim(slopes, device, 0, keepdims=False)
    own_value = lax.dynamic_index_in_dim(own_values, device, 0, keepdims=False)
    next_value = lax.dynamic_index_in_dim(next_values, device, 0, keepdims=False)
    return (offset + slope_part * own_value, next_value)


def on_device(initial_field, plane_coupling, line_coupling, source, shift_table, shift_index):
    layer_count = initial_field.shape[0]
    layer_index = lax.broadcasted_iota(jnp.int32, initial_field.shape, 0)
    current = initial_field
    for half_step in range(HALF):
        shift_value = lookup(shift_table, shift_index[half_step])
        padded = padded_2(current, (("gx", 1), ("gy", 2)), 1)
        beside_all = (
            padded[:, 2:, 1:-1] + padded[:, :-2, 1:-1] + padded[:, 1:-1, 2:] + padded[:, 1:-1, :-2]
        )
        explicit = current + shift_value * (plane_coupling * (beside_all - 4.0 * current) + source)
        scaled = shift_value * line_coupling
        zero_field = jnp.zeros_like(scaled)
        forcing = jnp.stack(
            [
                explicit,
                jnp.where(layer_index == 0, scaled, zero_field),
                jnp.where(layer_index == layer_count - 1, scaled, zero_field),
            ]
        )
        solved = local_solve(scaled, forcing)
        interior = solved[0]
        from_left = solved[1]
        from_right = solved[2]
        left_value, right_value = reduced_gathered(
            interior[0], interior[-1], from_left[0], from_left[-1], from_right[0], from_right[-1]
        )
        current = interior + left_value * from_left + right_value * from_right
    return current


def solution(mesh):
    in_specs = (
        P("gz", "gx", "gy"),
        P("gz", "gx", "gy"),
        P("gz", "gx", "gy"),
        P("gz", "gx", "gy"),
        P(),
        P(),
    )
    out_specs = P("gz", "gx", "gy")
    return jax.shard_map(
        on_device, mesh=mesh, in_specs=in_specs, out_specs=out_specs, check_vma=False
    )
```

profile of v0, /device:TPU:24, one launch (start us, length us, event | category | flops | bytes accessed | tf_op | source)
XLA Modules:
  0.0 167.4 jit_solution(2650618903797842976)
XLA Ops:
  0.0 1.2 fusion.198
  1.2 4.9 %collective-permute-start.3 = (f32[64,8,1]{2,1,0:T(8,128)S(1)}, f32[64,8,1]{2,1,0:T(8,128)S(1)}, u32[]{:S(2)}, u32[]{:S(2)}) collective-permute-start(f32[64,8,1]{2,1,0:T(8,128)S(1)} %get-tuple-element.1556), channel_id=1, source_target_pairs={{0,1},{1,2},{2,3},{3,4},{4,5},{5,6},{6,7},{7,8},{8,9},{9,10},{10,1... | collective-permute-start | bytes 6152 | tf_op jit(solution)/shard_map/ppermute | solution.py:41
  6.2 1.3 collective-permute-start
  7.5 3.0 %collective-permute-start.1 = (f32[64,1,128]{2,1,0:T(1,128)S(1)}, f32[64,1,128]{2,1,0:T(1,128)S(1)}, u32[]{:S(2)}, u32[]{:S(2)}) collective-permute-start(f32[64,1,128]{2,1,0:T(1,128)S(1)} %get-tuple-element.1557), channel_id=1, source_target_pairs={{0,32},{1,33},{2,34},{3,35},{4,36},{5,37},{6,38},{7,39},{8,40},{9,... | collective-permute-start | bytes 98312 | tf_op jit(solution)/shard_map/ppermute | solution.py:41
  10.6 3.3 %collective-permute-start.2 = (f32[64,8,1]{2,1,0:T(8,128)S(1)}, f32[64,8,1]{2,1,0:T(8,128)S(1)}, u32[]{:S(2)}, u32[]{:S(2)}) collective-permute-start(f32[64,8,1]{2,1,0:T(8,128)S(1)} %get-tuple-element.1555), channel_id=1, source_target_pairs={{1,0},{2,1},{3,2},{4,3},{5,4},{6,5},{7,6},{8,7},{9,8},{10,9},{11,1... | collective-permute-start | bytes 6152 | tf_op jit(solution)/shard_map/ppermute | solution.py:42
  14.6 0.7 copy-done.70
  15.2 3.1 %fusion.100 = (f32[]{:T(128)}, f32[]{:T(128)}, f32[]{:T(128)}, f32[]{:T(128)}) fusion(f32[8]{0:T(128)S(1)} %copy-done.70, s32[]{:T(128)} %bitcast, s32[]{:T(128)} %bitcast.17, s32[]{:T(128)} %bitcast.51, s32[]{:T(128)} %bitcast.34), kind=kLoop, calls=%fused_computation.414 | loop fusion | flops 92 | bytes 64 | tf_op jit(solution)/shard_map/reduce_sum | solution.py:55
  18.3 0.7 multiply_negate_fusion
  19.1 3.8 %add_add_fusion = (f32[64,8,128]{2,1,0:T(8,128)S(1)}, f32[64,8,128]{2,1,0:T(8,128)S(1)}, f32[64,8,128]{2,1,0:T(8,128)S(1)}, f32[64,8,128]{2,1,0:T(8,128)}, f32[6...) fusion(f32[64,8,128]{2,1,0:T(8,128)S(1)} %get-tuple-element.144, ...), kind=kLoop, calls=%fused_computation.250 | loop fusion | flops 1769472 | bytes 6537360 | tf_op jit(solution)/shard_map/add | solution.py:91
  23.2 3.2 %add_add_fusion.1 = (f32[64,8,128]{2,1,0:T(8,128)S(1)}, f32[64,8,128]{2,1,0:T(8,128)S(1)}, f32[64,8,128]{2,1,0:T(8,128)S(1)}, f32[64,8,128]{2,1,0:T(8,128)}, f32...) fusion(f32[64,8,128]{2,1,0:T(8,128)S(1)} %get-tuple-element.142, ...), kind=kLoop, calls=%fused_computation.281 | loop fusion | flops 1376256 | bytes 8077324 | tf_op jit(solution)/shard_map/add | solution.py:91
  37.6 0.9 fusion.133
  38.6 1.0 multiply_add_fusion.32
  39.6 1.0 multiply_add_fusion.26
  40.7 0.8 fusion.135
  41.8 1.0 fusion.96
  45.1 3.3 %all-to-all-start = ((f32[2,1,48,128]{3,2,1,0:T(8,128)}), f32[2,1,48,128]{3,2,1,0:T(8,128)S(1)}, u32[]{:S(2)}, u32[]{:S(2)}) async-start(f32[2,1,48,128]{3,2,1,0:T(8,128)} %broadcast_in_dim.193), calls=%async_computation | async-start | bytes 98304 | tf_op jit(solution)/shard_map/all_to_all | solution.py:17
  48.4 1.9 %pad_multiply_fusion = (f32[64,8,128]{2,1,0:T(8,128)}, f32[64,8,128]{2,1,0:T(8,128)}) fusion(f32[48,8,128]{2,1,0:T(8,128)} %get-tuple-element.1400, f32[48,8,128]{2,1,0:T(8,128)} %get-tuple-element.1404, f32[64,8,128]{2,1,0:T(8,128)S(1)} %get-tuple-element.1226), kind=kLoop, calls=%fused_computation.228 | loop fusion | flops 196608 | bytes 1179648 | tf_op jit(solution)/shard_map/mul | solution.py:94
  50.3 2.1 %all-to-all-done = f32[2,1,48,128]{3,2,1,0:T(8,128)S(1)} async-done(((f32[2,1,48,128]{3,2,1,0:T(8,128)}), f32[2,1,48,128]{3,2,1,0:T(8,128)S(1)}, u32[]{:S(2)}, u32[]{:S(2)}) %all-to-all-start) | async-done | bytes 49184 | tf_op jit(solution)/shard_map/all_to_all | solution.py:17
  53.0 4.0 %collective-permute-start.7 = (f32[64,8,1]{2,1,0:T(8,128)S(1)}, f32[64,8,1]{2,1,0:T(8,128)S(1)}, u32[]{:S(2)}, u32[]{:S(2)}) collective-permute-start(f32[64,8,1]{2,1,0:T(8,128)S(1)} %get-tuple-element.1522), channel_id=1, source_target_pairs={{0,1},{1,2},{2,3},{3,4},{4,5},{5,6},{6,7},{7,8},{8,9},{9,10},{10,1... | collective-permute-start | bytes 6152 | tf_op jit(solution)/shard_map/ppermute | solution.py:41
  57.0 1.3 collective-permute-start.4
  58.3 3.0 %collective-permute-start.5 = (f32[64,1,128]{2,1,0:T(1,128)S(1)}, f32[64,1,128]{2,1,0:T(1,128)S(1)}, u32[]{:S(2)}, u32[]{:S(2)}) collective-permute-start(f32[64,1,128]{2,1,0:T(1,128)S(1)} %get-tuple-element.1523), channel_id=1, source_target_pairs={{0,32},{1,33},{2,34},{3,35},{4,36},{5,37},{6,38},{7,39},{8,40},{9,... | collective-permute-start | bytes 98312 | tf_op jit(solution)/shard_map/ppermute | solution.py:41
  61.4 4.2 %collective-permute-start.6 = (f32[64,8,1]{2,1,0:T(8,128)S(1)}, f32[64,8,1]{2,1,0:T(8,128)S(1)}, u32[]{:S(2)}, u32[]{:S(2)}) collective-permute-start(f32[64,8,1]{2,1,0:T(8,128)S(1)} %get-tuple-element.1521), channel_id=1, source_target_pairs={{1,0},{2,1},{3,2},{4,3},{5,4},{6,5},{7,6},{8,7},{9,8},{10,9},{11,1... | collective-permute-start | bytes 6152 | tf_op jit(solution)/shard_map/ppermute | solution.py:42
  65.6 0.8 fusion.134
  66.4 7.3 %collective-permute-done.6 = f32[64,8,1]{2,1,0:T(8,128)S(1)} collective-permute-done((f32[64,8,1]{2,1,0:T(8,128)S(1)}, f32[64,8,1]{2,1,0:T(8,128)S(1)}, u32[]{:S(2)}, u32[]{:S(2)}) %collective-permute-start.6) | collective-permute-done | bytes 2080 | tf_op jit(solution)/shard_map/ppermute | solution.py:42
  73.7 1.0 fusion.81
  74.9 0.8 copy-done.59
  76.1 0.8 copy-done.21
  77.3 0.8 copy-done.25
  78.5 0.8 copy-done.49
  79.6 0.8 copy-done.35
  80.8 0.9 copy-done.64
  82.6 3.5 %all-to-all-start.1 = ((f32[2,1,48,128]{3,2,1,0:T(8,128)}), f32[2,1,48,128]{3,2,1,0:T(8,128)S(1)}, u32[]{:S(2)}, u32[]{:S(2)}) async-start(f32[2,1,48,128]{3,2,1,0:T(8,128)} %broadcast_in_dim.194), calls=%async_computation.1 | async-start | bytes 98304 | tf_op jit(solution)/shard_map/all_to_all | solution.py:17
  86.1 1.8 %pad_multiply_fusion.1 = (f32[64,8,128]{2,1,0:T(8,128)}, f32[64,8,128]{2,1,0:T(8,128)S(1)}) fusion(f32[48,8,128]{2,1,0:T(8,128)} %get-tuple-element.1402, f32[48,8,128]{2,1,0:T(8,128)} %get-tuple-element.1403, f32[64,8,128]{2,1,0:T(8,128)S(1)} %get-tuple-element.1224), kind=kLoop, calls=%fused_computation.231 | loop fusion | flops 196608 | bytes 1179648 | tf_op jit(solution)/shard_map/mul | solution.py:93
  87.9 2.1 %all-to-all-done.1 = f32[2,1,48,128]{3,2,1,0:T(8,128)S(1)} async-done(((f32[2,1,48,128]{3,2,1,0:T(8,128)}), f32[2,1,48,128]{3,2,1,0:T(8,128)S(1)}, u32[]{:S(2)}, u32[]{:S(2)}) %all-to-all-start.1) | async-done | bytes 49184 | tf_op jit(solution)/shard_map/all_to_all | solution.py:17
  90.5 8.3 %collective-permute-start.11 = (f32[64,8,1]{2,1,0:T(8,128)S(1)}, f32[64,8,1]{2,1,0:T(8,128)S(1)}, u32[]{:S(2)}, u32[]{:S(2)}) collective-permute-start(f32[64,8,1]{2,1,0:T(8,128)S(1)} %get-tuple-element.1488), channel_id=1, source_target_pairs={{0,1},{1,2},{2,3},{3,4},{4,5},{5,6},{6,7},{7,8},{8,9},{9,10},{10,1... | collective-permute-start | bytes 6152 | tf_op jit(solution)/shard_map/ppermute | solution.py:41
  98.8 1.3 collective-permute-start.8
  100.1 3.0 %collective-permute-start.9 = (f32[64,1,128]{2,1,0:T(1,128)S(1)}, f32[64,1,128]{2,1,0:T(1,128)S(1)}, u32[]{:S(2)}, u32[]{:S(2)}) collective-permute-start(f32[64,1,128]{2,1,0:T(1,128)S(1)} %get-tuple-element.1489), channel_id=1, source_target_pairs={{0,32},{1,33},{2,34},{3,35},{4,36},{5,37},{6,38},{7,39},{8,40},{9,... | collective-permute-start | bytes 98312 | tf_op jit(solution)/shard_map/ppermute | solution.py:41
  103.1 1.9 %collective-permute-start.10 = (f32[64,8,1]{2,1,0:T(8,128)S(1)}, f32[64,8,1]{2,1,0:T(8,128)S(1)}, u32[]{:S(2)}, u32[]{:S(2)}) collective-permute-start(f32[64,8,1]{2,1,0:T(8,128)S(1)} %get-tuple-element.1487), channel_id=1, source_target_pairs={{1,0},{2,1},{3,2},{4,3},{5,4},{6,5},{7,6},{8,7},{9,8},{10,9},{11,1... | collective-permute-start | bytes 6152 | tf_op jit(solution)/shard_map/ppermute | solution.py:42
  105.1 0.8 multiply_add_fusion.21
  105.9 8.2 %collective-permute-done.10 = f32[64,8,1]{2,1,0:T(8,128)S(1)} collective-permute-done((f32[64,8,1]{2,1,0:T(8,128)S(1)}, f32[64,8,1]{2,1,0:T(8,128)S(1)}, u32[]{:S(2)}, u32[]{:S(2)}) %collective-permute-start.10) | collective-permute-done | bytes 2080 | tf_op jit(solution)/shard_map/ppermute | solution.py:42
  114.1 1.0 fusion.66
  115.3 0.8 copy-done.57
  116.5 0.8 copy-done.11
  117.7 0.8 copy-done.17
  118.9 0.8 copy-done.45
  120.0 0.8 copy-done.31
  121.1 0.9 copy-done.61
  123.0 3.3 %all-to-all-start.2 = ((f32[2,1,48,128]{3,2,1,0:T(8,128)}), f32[2,1,48,128]{3,2,1,0:T(8,128)S(1)}, u32[]{:S(2)}, u32[]{:S(2)}) async-start(f32[2,1,48,128]{3,2,1,0:T(8,128)} %broadcast_in_dim.195), calls=%async_computation.2 | async-start | bytes 98304 | tf_op jit(solution)/shard_map/all_to_all | solution.py:17
  126.4 0.9 copy-done.54
  127.3 3.0 %all-to-all-done.2 = f32[2,1,48,128]{3,2,1,0:T(8,128)S(1)} async-done(((f32[2,1,48,128]{3,2,1,0:T(8,128)}), f32[2,1,48,128]{3,2,1,0:T(8,128)S(1)}, u32[]{:S(2)}, u32[]{:S(2)}) %all-to-all-start.2) | async-done | bytes 49184 | tf_op jit(solution)/shard_map/all_to_all | solution.py:17
  130.8 4.9 %collective-permute-start.15 = (f32[64,8,1]{2,1,0:T(8,128)S(1)}, f32[64,8,1]{2,1,0:T(8,128)S(1)}, u32[]{:S(2)}, u32[]{:S(2)}) collective-permute-start(f32[64,8,1]{2,1,0:T(8,128)S(1)} %get-tuple-element.1444), channel_id=1, source_target_pairs={{0,1},{1,2},{2,3},{3,4},{4,5},{5,6},{6,7},{7,8},{8,9},{9,10},{10,1... | collective-permute-start | bytes 6152 | tf_op jit(solution)/shard_map/ppermute | solution.py:41
  135.8 1.3 collective-permute-start.12
  137.1 3.0 %collective-permute-start.13 = (f32[64,1,128]{2,1,0:T(1,128)S(1)}, f32[64,1,128]{2,1,0:T(1,128)S(1)}, u32[]{:S(2)}, u32[]{:S(2)}) collective-permute-start(f32[64,1,128]{2,1,0:T(1,128)S(1)} %get-tuple-element.1445), channel_id=1, source_target_pairs={{0,32},{1,33},{2,34},{3,35},{4,36},{5,37},{6,38},{7,39},{8,40},{9,... | collective-permute-start | bytes 98312 | tf_op jit(solution)/shard_map/ppermute | solution.py:41
  140.1 3.3 %collective-permute-start.14 = (f32[64,8,1]{2,1,0:T(8,128)S(1)}, f32[64,8,1]{2,1,0:T(8,128)S(1)}, u32[]{:S(2)}, u32[]{:S(2)}) collective-permute-start(f32[64,8,1]{2,1,0:T(8,128)S(1)} %get-tuple-element.1443), channel_id=1, source_target_pairs={{1,0},{2,1},{3,2},{4,3},{5,4},{6,5},{7,6},{8,7},{9,8},{10,9},{11,1... | collective-permute-start | bytes 6152 | tf_op jit(solution)/shard_map/ppermute | solution.py:42
  143.5 7.6 %collective-permute-done.14 = f32[64,8,1]{2,1,0:T(8,128)S(1)} collective-permute-done((f32[64,8,1]{2,1,0:T(8,128)S(1)}, f32[64,8,1]{2,1,0:T(8,128)S(1)}, u32[]{:S(2)}, u32[]{:S(2)}) %collective-permute-start.14) | collective-permute-done | bytes 2080 | tf_op jit(solution)/shard_map/ppermute | solution.py:42
  151.1 1.0 fusion.51
  152.4 0.8 copy-done.55
  153.6 0.8 copy-done.5
  154.7 0.8 copy-done.7
  155.9 0.8 copy-done.41
  157.1 0.8 copy-done.29
  159.0 3.3 %all-to-all-start.3 = ((f32[2,1,48,128]{3,2,1,0:T(8,128)}), f32[2,1,48,128]{3,2,1,0:T(8,128)S(1)}, u32[]{:S(2)}, u32[]{:S(2)}) async-start(f32[2,1,48,128]{3,2,1,0:T(8,128)} %broadcast_in_dim.196), calls=%async_computation.3 | async-start | bytes 98304 | tf_op jit(solution)/shard_map/all_to_all | solution.py:17
  162.3 4.0 %all-to-all-done.3 = f32[2,1,48,128]{3,2,1,0:T(8,128)S(1)} async-done(((f32[2,1,48,128]{3,2,1,0:T(8,128)}), f32[2,1,48,128]{3,2,1,0:T(8,128)S(1)}, u32[]{:S(2)}, u32[]{:S(2)}) %all-to-all-start.3) | async-done | bytes 49184 | tf_op jit(solution)/shard_map/all_to_all | solution.py:17
  166.6 0.7 fusion.41
  (419 shorter events, 24.4 us)
Async XLA Ops:
  0.0 6.2 %copy-start.2 = (f32[64,8,128]{2,1,0:T(8,128)S(1)}, f32[64,8,128]{2,1,0:T(8,128)}, u32[]{:S(2)}) copy-start(f32[64,8,128]{2,1,0:T(8,128)} %param.22) | copy-start | bytes 786436
  0.0 18.3 %copy-start.3 = (f32[64,8,128]{2,1,0:T(8,128)S(1)}, f32[64,8,128]{2,1,0:T(8,128)}, u32[]{:S(2)}) copy-start(f32[64,8,128]{2,1,0:T(8,128)} %param.24) | copy-start | bytes 786436
  1.2 40.2 %collective-permute-start.3 = (f32[64,8,1]{2,1,0:T(8,128)S(1)}, f32[64,8,1]{2,1,0:T(8,128)S(1)}, u32[]{:S(2)}, u32[]{:S(2)}) collective-permute-start(f32[64,8,1]{2,1,0:T(8,128)S(1)} %get-tuple-element.1556), channel_id=1, source_target_pairs={{0,1},{1,2},{2,3},{3,4},{4,5},{5,6},{6,7},{7,8},{8,9},{9,10},{10,1... | collective-permute-start | bytes 6152 | tf_op jit(solution)/shard_map/ppermute | solution.py:41
  6.2 35.2 %collective-permute-start = (f32[64,1,128]{2,1,0:T(1,128)S(1)}, f32[64,1,128]{2,1,0:T(1,128)S(1)}, u32[]{:S(2)}, u32[]{:S(2)}) collective-permute-start(f32[64,1,128]{2,1,0:T(1,128)S(1)} %get-tuple-element.1558), channel_id=1, source_target_pairs={{32,0},{33,1},{34,2},{35,3},{36,4},{37,5},{38,6},{39,7},{40,8},{41... | collective-permute-start | bytes 98312 | tf_op jit(solution)/shard_map/ppermute | solution.py:42
  7.5 33.9 %collective-permute-start.1 = (f32[64,1,128]{2,1,0:T(1,128)S(1)}, f32[64,1,128]{2,1,0:T(1,128)S(1)}, u32[]{:S(2)}, u32[]{:S(2)}) collective-permute-start(f32[64,1,128]{2,1,0:T(1,128)S(1)} %get-tuple-element.1557), channel_id=1, source_target_pairs={{0,32},{1,33},{2,34},{3,35},{4,36},{5,37},{6,38},{7,39},{8,40},{9,... | collective-permute-start | bytes 98312 | tf_op jit(solution)/shard_map/ppermute | solution.py:41
  10.6 3.3 %copy-start.69 = (s32[4]{0:T(128)S(1)}, s32[4]{0:T(128)}, u32[]{:S(2)}) copy-start(s32[4]{0:T(128)} %param.27) | copy-start | bytes 52
  10.6 30.8 %collective-permute-start.2 = (f32[64,8,1]{2,1,0:T(8,128)S(1)}, f32[64,8,1]{2,1,0:T(8,128)S(1)}, u32[]{:S(2)}, u32[]{:S(2)}) collective-permute-start(f32[64,8,1]{2,1,0:T(8,128)S(1)} %get-tuple-element.1555), channel_id=1, source_target_pairs={{1,0},{2,1},{3,2},{4,3},{5,4},{6,5},{7,6},{8,7},{9,8},{10,9},{11,1... | collective-permute-start | bytes 6152 | tf_op jit(solution)/shard_map/ppermute | solution.py:42
  37.6 3.0 %copy-start.40 = (f32[64,8,128]{2,1,0:T(8,128)}, f32[64,8,128]{2,1,0:T(8,128)S(1)}, u32[]{:S(2)}) copy-start(f32[64,8,128]{2,1,0:T(8,128)S(1)} %get-tuple-element.1227) | copy-start | bytes 786436
  38.5 2.1 %copy-start.42 = (f32[64,8,128]{2,1,0:T(8,128)}, f32[64,8,128]{2,1,0:T(8,128)S(1)}, u32[]{:S(2)}) copy-start(f32[64,8,128]{2,1,0:T(8,128)S(1)} %get-tuple-element.1225) | copy-start | bytes 786436
  40.6 1.0 copy-start
  40.6 1.2 copy-start.1
  45.1 7.3 %all-to-all-start = ((f32[2,1,48,128]{3,2,1,0:T(8,128)}), f32[2,1,48,128]{3,2,1,0:T(8,128)S(1)}, u32[]{:S(2)}, u32[]{:S(2)}) async-start(f32[2,1,48,128]{3,2,1,0:T(8,128)} %broadcast_in_dim.193), calls=%async_computation | async-start | bytes 98304 | tf_op jit(solution)/shard_map/all_to_all | solution.py:17
  53.0 13.4 %collective-permute-start.7 = (f32[64,8,1]{2,1,0:T(8,128)S(1)}, f32[64,8,1]{2,1,0:T(8,128)S(1)}, u32[]{:S(2)}, u32[]{:S(2)}) collective-permute-start(f32[64,8,1]{2,1,0:T(8,128)S(1)} %get-tuple-element.1522), channel_id=1, source_target_pairs={{0,1},{1,2},{2,3},{3,4},{4,5},{5,6},{6,7},{7,8},{8,9},{9,10},{10,1... | collective-permute-start | bytes 6152 | tf_op jit(solution)/shard_map/ppermute | solution.py:41
  57.0 16.6 %collective-permute-start.4 = (f32[64,1,128]{2,1,0:T(1,128)S(1)}, f32[64,1,128]{2,1,0:T(1,128)S(1)}, u32[]{:S(2)}, u32[]{:S(2)}) collective-permute-start(f32[64,1,128]{2,1,0:T(1,128)S(1)} %get-tuple-element.1524), channel_id=1, source_target_pairs={{32,0},{33,1},{34,2},{35,3},{36,4},{37,5},{38,6},{39,7},{40,8},{41... | collective-permute-start | bytes 98312 | tf_op jit(solution)/shard_map/ppermute | solution.py:42
  58.3 15.3 %collective-permute-start.5 = (f32[64,1,128]{2,1,0:T(1,128)S(1)}, f32[64,1,128]{2,1,0:T(1,128)S(1)}, u32[]{:S(2)}, u32[]{:S(2)}) collective-permute-start(f32[64,1,128]{2,1,0:T(1,128)S(1)} %get-tuple-element.1523), channel_id=1, source_target_pairs={{0,32},{1,33},{2,34},{3,35},{4,36},{5,37},{6,38},{7,39},{8,40},{9,... | collective-permute-start | bytes 98312 | tf_op jit(solution)/shard_map/ppermute | solution.py:41
  61.4 12.3 %collective-permute-start.6 = (f32[64,8,1]{2,1,0:T(8,128)S(1)}, f32[64,8,1]{2,1,0:T(8,128)S(1)}, u32[]{:S(2)}, u32[]{:S(2)}) collective-permute-start(f32[64,8,1]{2,1,0:T(8,128)S(1)} %get-tuple-element.1521), channel_id=1, source_target_pairs={{1,0},{2,1},{3,2},{4,3},{5,4},{6,5},{7,6},{8,7},{9,8},{10,9},{11,1... | collective-permute-start | bytes 6152 | tf_op jit(solution)/shard_map/ppermute | solution.py:42
  66.4 8.3 %copy-start.14 = (f32[1,64,8,128]{3,2,1,0:T(8,128)S(1)}, f32[1,64,8,128]{3,2,1,0:T(8,128)}, u32[]{:S(2)}) copy-start(f32[1,64,8,128]{3,2,1,0:T(8,128)} %get-tuple-element.1431) | copy-start | bytes 786436
  66.4 8.3 %copy-start.15 = (f32[1,64,8,128]{3,2,1,0:T(8,128)S(1)}, f32[1,64,8,128]{3,2,1,0:T(8,128)}, u32[]{:S(2)}) copy-start(f32[1,64,8,128]{3,2,1,0:T(8,128)} %get-tuple-element.1435) | copy-start | bytes 786436
  74.8 1.0 copy-start.59
  74.8 1.0 copy-start.60
  76.0 1.0 copy-start.21
  76.0 1.0 copy-start.23
  77.2 1.0 copy-start.27
  78.4 1.0 copy-start.49
  78.4 1.0 copy-start.51
  79.5 1.0 copy-start.37
  80.7 1.0 copy-start.65
  80.7 1.1 copy-start.66
  82.6 7.3 %all-to-all-start.1 = ((f32[2,1,48,128]{3,2,1,0:T(8,128)}), f32[2,1,48,128]{3,2,1,0:T(8,128)S(1)}, u32[]{:S(2)}, u32[]{:S(2)}) async-start(f32[2,1,48,128]{3,2,1,0:T(8,128)} %broadcast_in_dim.194), calls=%async_computation.1 | async-start | bytes 98304 | tf_op jit(solution)/shard_map/all_to_all | solution.py:17
  87.8 17.2 %copy-start.38 = (f32[64,8,128]{2,1,0:T(8,128)}, f32[64,8,128]{2,1,0:T(8,128)S(1)}, u32[]{:S(2)}) copy-start(f32[64,8,128]{2,1,0:T(8,128)S(1)} %get-tuple-element.1221) | copy-start | bytes 786436
  90.3 14.8 %copy-start.28 = (f32[64,8,128]{2,1,0:T(8,128)S(1)}, f32[64,8,128]{2,1,0:T(8,128)}, u32[]{:S(2)}) copy-start(f32[64,8,128]{2,1,0:T(8,128)} %get-tuple-element.1223) | copy-start | bytes 786436
  90.3 14.8 %copy-start.67 = (f32[48,8,128]{2,1,0:T(8,128)S(1)}, f32[48,8,128]{2,1,0:T(8,128)}, u32[]{:S(2)}) copy-start(f32[48,8,128]{2,1,0:T(8,128)} %get-tuple-element.1399) | copy-start | bytes 589828
  90.3 14.8 %copy-start.68 = (f32[48,8,128]{2,1,0:T(8,128)S(1)}, f32[48,8,128]{2,1,0:T(8,128)}, u32[]{:S(2)}) copy-start(f32[48,8,128]{2,1,0:T(8,128)} %get-tuple-element.1401) | copy-start | bytes 589828
  90.5 15.4 %collective-permute-start.11 = (f32[64,8,1]{2,1,0:T(8,128)S(1)}, f32[64,8,1]{2,1,0:T(8,128)S(1)}, u32[]{:S(2)}, u32[]{:S(2)}) collective-permute-start(f32[64,8,1]{2,1,0:T(8,128)S(1)} %get-tuple-element.1488), channel_id=1, source_target_pairs={{0,1},{1,2},{2,3},{3,4},{4,5},{5,6},{6,7},{7,8},{8,9},{9,10},{10,1... | collective-permute-start | bytes 6152 | tf_op jit(solution)/shard_map/ppermute | solution.py:41
  98.8 15.3 %collective-permute-start.8 = (f32[64,1,128]{2,1,0:T(1,128)S(1)}, f32[64,1,128]{2,1,0:T(1,128)S(1)}, u32[]{:S(2)}, u32[]{:S(2)}) collective-permute-start(f32[64,1,128]{2,1,0:T(1,128)S(1)} %get-tuple-element.1490), channel_id=1, source_target_pairs={{32,0},{33,1},{34,2},{35,3},{36,4},{37,5},{38,6},{39,7},{40,8},{41... | collective-permute-start | bytes 98312 | tf_op jit(solution)/shard_map/ppermute | solution.py:42
  100.1 14.0 %collective-permute-start.9 = (f32[64,1,128]{2,1,0:T(1,128)S(1)}, f32[64,1,128]{2,1,0:T(1,128)S(1)}, u32[]{:S(2)}, u32[]{:S(2)}) collective-permute-start(f32[64,1,128]{2,1,0:T(1,128)S(1)} %get-tuple-element.1489), channel_id=1, source_target_pairs={{0,32},{1,33},{2,34},{3,35},{4,36},{5,37},{6,38},{7,39},{8,40},{9,... | collective-permute-start | bytes 98312 | tf_op jit(solution)/shard_map/ppermute | solution.py:41
  103.1 11.0 %collective-permute-start.10 = (f32[64,8,1]{2,1,0:T(8,128)S(1)}, f32[64,8,1]{2,1,0:T(8,128)S(1)}, u32[]{:S(2)}, u32[]{:S(2)}) collective-permute-start(f32[64,8,1]{2,1,0:T(8,128)S(1)} %get-tuple-element.1487), channel_id=1, source_target_pairs={{1,0},{2,1},{3,2},{4,3},{5,4},{6,5},{7,6},{8,7},{9,8},{10,9},{11,1... | collective-permute-start | bytes 6152 | tf_op jit(solution)/shard_map/ppermute | solution.py:42
  115.2 1.0 copy-start.58
  116.4 1.0 copy-start.13
  117.6 1.0 copy-start.17
  117.6 1.0 copy-start.19
  118.7 1.0 copy-start.47
  119.9 1.0 copy-start.33
  121.0 1.0 copy-start.61
  121.1 1.0 copy-start.62
  121.1 1.1 copy-start.63
  122.2 4.1 %copy-start.52 = (f32[64,8,128]{2,1,0:T(8,128)S(1)}, f32[64,8,128]{2,1,0:T(8,128)}, u32[]{:S(2)}) copy-start(f32[64,8,128]{2,1,0:T(8,128)} %multiply_add_fusion.21) | copy-start | bytes 786436
  123.0 7.3 %all-to-all-start.2 = ((f32[2,1,48,128]{3,2,1,0:T(8,128)}), f32[2,1,48,128]{3,2,1,0:T(8,128)S(1)}, u32[]{:S(2)}, u32[]{:S(2)}) async-start(f32[2,1,48,128]{3,2,1,0:T(8,128)} %broadcast_in_dim.195), calls=%async_computation.2 | async-start | bytes 98304 | tf_op jit(solution)/shard_map/all_to_all | solution.py:17
  126.3 1.0 copy-start.54
  126.3 1.0 copy-start.53
  130.8 12.7 %collective-permute-start.15 = (f32[64,8,1]{2,1,0:T(8,128)S(1)}, f32[64,8,1]{2,1,0:T(8,128)S(1)}, u32[]{:S(2)}, u32[]{:S(2)}) collective-permute-start(f32[64,8,1]{2,1,0:T(8,128)S(1)} %get-tuple-element.1444), channel_id=1, source_target_pairs={{0,1},{1,2},{2,3},{3,4},{4,5},{5,6},{6,7},{7,8},{8,9},{9,10},{10,1... | collective-permute-start | bytes 6152 | tf_op jit(solution)/shard_map/ppermute | solution.py:41
  135.8 15.3 %collective-permute-start.12 = (f32[64,1,128]{2,1,0:T(1,128)S(1)}, f32[64,1,128]{2,1,0:T(1,128)S(1)}, u32[]{:S(2)}, u32[]{:S(2)}) collective-permute-start(f32[64,1,128]{2,1,0:T(1,128)S(1)} %get-tuple-element.1446), channel_id=1, source_target_pairs={{32,0},{33,1},{34,2},{35,3},{36,4},{37,5},{38,6},{39,7},{40,8},{41... | collective-permute-start | bytes 98312 | tf_op jit(solution)/shard_map/ppermute | solution.py:42
  137.1 14.0 %collective-permute-start.13 = (f32[64,1,128]{2,1,0:T(1,128)S(1)}, f32[64,1,128]{2,1,0:T(1,128)S(1)}, u32[]{:S(2)}, u32[]{:S(2)}) collective-permute-start(f32[64,1,128]{2,1,0:T(1,128)S(1)} %get-tuple-element.1445), channel_id=1, source_target_pairs={{0,32},{1,33},{2,34},{3,35},{4,36},{5,37},{6,38},{7,39},{8,40},{9,... | collective-permute-start | bytes 98312 | tf_op jit(solution)/shard_map/ppermute | solution.py:41
  140.1 11.0 %collective-permute-start.14 = (f32[64,8,1]{2,1,0:T(8,128)S(1)}, f32[64,8,1]{2,1,0:T(8,128)S(1)}, u32[]{:S(2)}, u32[]{:S(2)}) collective-permute-start(f32[64,8,1]{2,1,0:T(8,128)S(1)} %get-tuple-element.1443), channel_id=1, source_target_pairs={{1,0},{2,1},{3,2},{4,3},{5,4},{6,5},{7,6},{8,7},{9,8},{10,9},{11,1... | collective-permute-start | bytes 6152 | tf_op jit(solution)/shard_map/ppermute | solution.py:42
  152.2 1.0 copy-start.55
  152.3 1.0 copy-start.56
  153.5 1.0 copy-start.5
  154.6 1.0 copy-start.7
  154.6 1.0 copy-start.9
  155.8 1.0 copy-start.41
  155.8 1.0 copy-start.43
  156.9 1.0 copy-start.29
  157.0 1.0 copy-start.39
  159.0 7.3 %all-to-all-start.3 = ((f32[2,1,48,128]{3,2,1,0:T(8,128)}), f32[2,1,48,128]{3,2,1,0:T(8,128)S(1)}, u32[]{:S(2)}, u32[]{:S(2)}) async-start(f32[2,1,48,128]{3,2,1,0:T(8,128)} %broadcast_in_dim.196), calls=%async_computation.3 | async-start | bytes 98304 | tf_op jit(solution)/shard_map/all_to_all | solution.py:17
  (27 other events, 20.8 us)
where the time goes:
time: 169 us; the launch traced here: 167 us
  starting transfers between devices  65.5 us (39%)
  local copies, waits for them, and re-layouts  35.3 us (21%)
  waiting for transfers between devices  34.2 us (20%)
  other arithmetic  29.5 us (17%)
  between operations  2.33 us (1%)
    ppermute x8, starting transfers between devices, padded_2(): lax.ppermute(last, axis, up)  34.3 us
    unnamed x162, local copies, waits for them, and re-layouts  23.9 us
    ppermute x8, waiting for transfers between devices, padded_2(): lax.ppermute(first, axis, [(b, a) for a, b in up])  23.1 us
    ppermute x8, starting transfers between devices, padded_2(): lax.ppermute(first, axis, [(b, a) for a, b in up])  17.9 us
    all_to_all x4, starting transfers between devices, copy_for_each(): return lax.all_to_all(copies, axis, split_axis=0, concat_axis=0, tiled=True)  13.3 us
    add x22, other arithmetic, local_solve(): main_band + left_factor * upper_before + right_factor * lower_after  11.1 us
    all_to_all x4, waiting for transfers between devices, copy_for_each(): return lax.all_to_all(copies, axis, split_axis=0, concat_axis=0, tiled=True)  11.1 us
    slice x60, local copies, waits for them, and re-layouts, from_below(): lax.slice_in_dim(values, 0, values.shape[which_axis] - stride, axis=which...  4.73 us
  transfers between devices with their start and end apart: 20, of which 7 were waited for; matrix products, arithmetic and copies ran while one was open for 15% of the time, Pallas kernels for 0%

commit v1 on v0

v1 whole, which is shorter than its diff:
```python
import functools
import jax
import jax.numpy as jnp
from jax import lax
from jax.experimental import pallas as pl
from jax.experimental.pallas import tpu as pltpu
from jax.sharding import PartitionSpec as P

HALF = 4
ROWS = 8
LANES = 128
UNROLL = 4
FIELD, PLANE, LINE, SOURCE = range(4)
MESH = pl.DeviceIdType.MESH


def kernel(
    columns,
    field_hbm, plane_hbm, line_hbm, source_hbm, table_hbm, index_hbm,
    out_hbm,
    table, index, block, theta, weight, inverse, state, packed, halo,
    pivots, pivots_in, mixed, planes, planes_in, result,
    local_sem, scalar_sem, out_sem,
    swap_send, swap_recv, far_send, far_recv, pass_send, pass_recv,
    pivot_send, pivot_recv, plane_send, plane_recv,
):
    layers = field_hbm.shape[0]
    gz, gx, gy = lax.axis_index("gz"), lax.axis_index("gx"), lax.axis_index("gy")
    has_left, has_right = gy > 0, gy < columns - 1
    lane = lax.broadcasted_iota(jnp.int32, (ROWS, LANES), 1)
    row = lax.broadcasted_iota(jnp.int32, (ROWS, LANES), 0)
    zero = jnp.zeros((ROWS, LANES), jnp.float32)
    one = jnp.ones((ROWS, LANES), jnp.float32)

    def layer(k):
        return gz * (layers - 1) + (1 - 2 * gz) * k

    loads = [
        pltpu.make_async_copy(source, block.at[a, gx], local_sem.at[a])
        for a, source in enumerate((field_hbm, plane_hbm, line_hbm, source_hbm))
    ]
    scalars = [
        pltpu.make_async_copy(table_hbm, table, scalar_sem.at[0]),
        pltpu.make_async_copy(index_hbm, index, scalar_sem.at[1]),
    ]
    for copy in scalars + loads:
        copy.start()

    barrier = pltpu.get_barrier_semaphore()
    pl.semaphore_signal(barrier, inc=1, device_id={"gx": 1 - gx}, device_id_type=MESH)
    pl.semaphore_signal(barrier, inc=1, device_id={"gz": 1 - gz}, device_id_type=MESH)

    @pl.when(has_left)
    def _():
        pl.semaphore_signal(barrier, inc=1, device_id={"gy": gy - 1}, device_id_type=MESH)

    @pl.when(has_right)
    def _():
        pl.semaphore_signal(barrier, inc=1, device_id={"gy": gy + 1}, device_id_type=MESH)

    for copy in scalars:
        copy.wait()
    shifts = [jnp.full((ROWS, LANES), table[index[h]], jnp.float32) for h in range(HALF)]
    inverses = [1.0 / s for s in shifts]

    for copy in loads:
        copy.wait()

    slots = LANES // 8
    groups = layers // (2 * slots)

    def pack(j, _):
        for a in range(4):
            left, right = zero, zero
            for b in range(2):
                for i in range(slots):
                    p = 8 * i + 4 * b
                    moved = block[a, gx, j * 2 * slots + b * slots + i]
                    if p:
                        moved = pltpu.roll(moved, p, 1)
                    at = lane // 4
                    right = jnp.where(at == p // 4, moved, right)
                    left = jnp.where(at == (p // 4 - 1) % 32, moved, left)
            packed[0, a * groups + j] = left
            packed[1, a * groups + j] = right
        return 0

    lax.fori_loop(0, groups, pack, 0)

    for side, missing in ((0, jnp.logical_not(has_left)), (1, jnp.logical_not(has_right))):
        @pl.when(missing)
        def _(side=side):
            for r in range(2):
                for a in range(4):
                    for j in range(groups):
                        halo[side, r, a * groups + j] = one * 1000.0 if a == LINE else zero

    def factor(q):
        def steps(t, carry):
            carry = list(carry)
            for s in range(UNROLL):
                k = layer(t * UNROLL + s)
                line = 1.0 / block[LINE, q, k]
                for h in range(HALF):
                    th, de = carry[2 * h], carry[2 * h + 1]
                    ratio = line * inverses[h]
                    w = ratio * th
                    de = de + w
                    new = th + de
                    theta[h, q, k] = th
                    weight[h, q, k] = w
                    inverse[h, q, k] = 1.0 / (new * th)
                    carry[2 * h], carry[2 * h + 1] = new, de
            return tuple(carry)

        end = lax.fori_loop(0, layers // UNROLL, steps, (one,) * (2 * HALF))
        for h in range(HALF):
            pivots[q, h, 0] = end[2 * h]
            pivots[q, h, 1] = end[2 * h + 1]

    factor(gx)

    signals = 2 + has_left.astype(jnp.int32) + has_right.astype(jnp.int32)
    pl.semaphore_wait(barrier, signals)

    def far(side):
        return pltpu.make_async_remote_copy(
            src_ref=packed.at[side],
            dst_ref=halo.at[side, gx],
            send_sem=far_send.at[side],
            recv_sem=far_recv.at[side],
            device_id={"gy": gy + 1 - 2 * side},
            device_id_type=MESH,
        )

    @pl.when(has_right)
    def _():
        far(0).start()

    @pl.when(has_left)
    def _():
        far(1).start()

    swaps = [
        pltpu.make_async_remote_copy(
            src_ref=block.at[a, gx],
            dst_ref=block.at[a, gx],
            send_sem=swap_send.at[a],
            recv_sem=swap_recv.at[a],
            device_id={"gx": 1 - gx},
            device_id_type=MESH,
        )
        for a in (LINE, FIELD, PLANE, SOURCE)
    ]
    for copy in swaps:
        copy.start()
    for copy in swaps:
        copy.wait_recv()
    factor(1 - gx)

    def pivot_copy(e):
        return pltpu.make_async_remote_copy(
            src_ref=pivots.at[pl.ds(2 * e, 2)],
            dst_ref=pivots_in.at[pl.ds(2 * e, 2)],
            send_sem=pivot_send.at[e],
            recv_sem=pivot_recv.at[e],
            device_id={"gz": 1 - gz},
            device_id_type=MESH,
        )

    pivot_copy(0).start()

    def passed(side):
        return pltpu.make_async_remote_copy(
            src_ref=halo.at[side, gx],
            dst_ref=halo.at[side, gx],
            send_sem=pass_send.at[side],
            recv_sem=pass_recv.at[side],
            device_id={"gx": 1 - gx},
            device_id_type=MESH,
        )

    for side, there in ((0, has_left), (1, has_right)):
        @pl.when(there)
        def _(side=side):
            far(side).wait_recv()
            passed(side).start()

    for side, there in ((0, has_left), (1, has_right)):
        @pl.when(there)
        def _(side=side):
            passed(side).wait_recv()

    odd = lax.rem(lane // 4, 2) == 1

    def unpack(j, _):
        for a in range(4):
            for r in range(2):
                left = halo[0, r, a * groups + j]
                right = halo[1, r, a * groups + j]
                for b in range(2):
                    both = jnp.where(odd, right, left) if b else jnp.where(odd, left, right)
                    for i in range(slots):
                        p = 8 * i + 4 * b
                        block[a, 2 + r, j * 2 * slots + b * slots + i] = (
                            pltpu.roll(both, LANES - p, 1) if p else both
                        )
        return 0

    lax.fori_loop(0, groups, unpack, 0)
    factor(2)
    factor(3)
    pivot_copy(1).start()
    pivot_copy(0).wait_recv()
    pivot_copy(1).wait_recv()
    for q in range(4):
        for h in range(HALF):
            last, step = pivots[q, h, 0], pivots[q, h, 1]
            other_last, other_step = pivots_in[q, h, 0], pivots_in[q, h, 1]
            before = last - step
            share = 1.0 / (before * other_step + step * other_last)
            mixed[q, h, 0] = other_last * share / before
            mixed[q, h, 1] = share

    first, final = lane == 0, lane == LANES - 1
    top, bottom = row == 0, row == ROWS - 1

    def spread(u):
        ups = [pltpu.roll(x, 1, 0) for x in u]
        downs = [pltpu.roll(x, ROWS - 1, 0) for x in u]
        lefts = [pltpu.roll(x, 1, 1) for x in u]
        rights = [pltpu.roll(x, LANES - 1, 1) for x in u]
        sums = []
        for q in range(4):
            r, twin = q % 2, (q + 2) % 4
            up = jnp.where(top, ups[q - 1] if r else zero, ups[q])
            down = jnp.where(bottom, zero if r else downs[q + 1], downs[q])
            left = jnp.where(first, lefts[twin], lefts[q])
            right = jnp.where(final, rights[twin], rights[q])
            sums.append((up + down) + (left + right))
        return sums

    def plane_copy(h):
        return pltpu.make_async_remote_copy(
            src_ref=planes.at[h],
            dst_ref=planes_in.at[h],
            send_sem=plane_send.at[h],
            recv_sem=plane_recv.at[h],
            device_id={"gz": 1 - gz},
            device_id_type=MESH,
        )

    ends = [zero] * 4
    for h in range(HALF):
        shift = shifts[h]

        def forward(t, total, h=h, shift=shift, ends=ends):
            total = list(total)
            for s in range(UNROLL):
                k = layer(t * UNROLL + s)
                if h == 0:
                    u = [block[FIELD, q, k] for q in range(4)]
                else:
                    u = [theta[h - 1, q, k] * (state[q, k] + ends[q]) for q in range(4)]
                beside = spread(u)
                for q in range(4):
                    flux = block[PLANE, q, k] * (beside[q] - 4.0 * u[q]) + block[SOURCE, q, k]
                    explicit = u[q] + shift * flux
                    total[q] = total[q] + weight[h, q, k] * explicit
                    state[q, k] = inverse[h, q, k] * total[q]
            return tuple(total)

        total = lax.fori_loop(0, layers // UNROLL, forward, (zero,) * 4)
        for q in range(4):
            planes[h, q] = total[q]
        plane_copy(h).start()

        def backward(t, later, h=h):
            later = list(later)
            for s in range(UNROLL):
                k = layer(layers - 1 - (t * UNROLL + s))
                for q in range(4):
                    here = state[q, k]
                    if s == 0:
                        here = jnp.where(t == 0, zero, here)
                    later[q] = later[q] + here
                    state[q, k] = later[q]
            return tuple(later)

        lax.fori_loop(0, layers // UNROLL, backward, (zero,) * 4)
        plane_copy(h).wait_recv()
        ends = [
            mixed[q, h, 0] * planes[h, q] + mixed[q, h, 1] * planes_in[h, q] for q in range(4)
        ]

    own_end = jnp.where(gx == 0, ends[0], ends[1])

    def finish(t, _):
        for s in range(UNROLL):
            k = t * UNROLL + s
            result[k] = theta[HALF - 1, gx, k] * (state[gx, k] + own_end)
        return 0

    lax.fori_loop(0, layers // UNROLL, finish, 0)
    store = pltpu.make_async_copy(result, out_hbm, out_sem)
    store.start()

    for copy in swaps:
        copy.wait_send()
    for side, there in ((0, has_left), (1, has_right)):
        @pl.when(there)
        def _(side=side):
            passed(side).wait_send()

    @pl.when(has_right)
    def _():
        far(0).wait_send()

    @pl.when(has_left)
    def _():
        far(1).wait_send()

    for e in range(2):
        pivot_copy(e).wait_send()
    for h in range(HALF):
        plane_copy(h).wait_send()
    store.wait()


def on_device(columns, field, plane, line, source, table, index):
    layers = field.shape[0]
    tile = (ROWS, LANES)
    f32 = jnp.float32
    groups = layers // 32
    dma = pltpu.SemaphoreType.DMA
    return pl.pallas_call(
        functools.partial(kernel, columns),
        out_shape=jax.ShapeDtypeStruct(field.shape, f32),
        in_specs=[pl.BlockSpec(memory_space=pltpu.HBM)] * 6,
        out_specs=pl.BlockSpec(memory_space=pltpu.HBM),
        scratch_shapes=[
            pltpu.SMEM(table.shape, f32),
            pltpu.SMEM(index.shape, jnp.int32),
            pltpu.VMEM((4, 4, layers, *tile), f32),
            pltpu.VMEM((HALF, 4, layers, *tile), f32),
            pltpu.VMEM((HALF, 4, layers, *tile), f32),
            pltpu.VMEM((HALF, 4, layers, *tile), f32),
            pltpu.VMEM((4, layers, *tile), f32),
            pltpu.VMEM((2, 4 * groups, *tile), f32),
            pltpu.VMEM((2, 2, 4 * groups, *tile), f32),
            pltpu.VMEM((4, HALF, 2, *tile), f32),
            pltpu.VMEM((4, HALF, 2, *tile), f32),
            pltpu.VMEM((4, HALF, 2, *tile), f32),
            pltpu.VMEM((HALF, 4, *tile), f32),
            pltpu.VMEM((HALF, 4, *tile), f32),
            pltpu.VMEM((layers, *tile), f32),
            dma((4,)), dma((2,)), dma,
            dma((4,)), dma((4,)), dma((2,)), dma((2,)), dma((2,)), dma((2,)),
            dma((2,)), dma((2,)), dma((HALF,)), dma((HALF,)),
        ],
        compiler_params=pltpu.CompilerParams(
            collective_id=0, has_side_effects=True, vmem_limit_bytes=67043328
        ),
    )(field, plane, line, source, table, index)


def solution(mesh):
    spec = P("gz", "gx", "gy")
    return jax.shard_map(
        functools.partial(on_device, mesh.shape["gy"]),
        mesh=mesh,
        in_specs=(spec, spec, spec, spec, P(), P()),
        out_specs=spec,
        check_vma=False,
    )
```

time: 169 us -> 47 us (0.28)
  the two profiles are of different devices: /device:TPU:24 before, /device:TPU:96 now
where the time goes in v1:
time: 47 us; the launch traced here: 46.8 us
  Pallas kernels  45.1 us (96%)
  local copies, waits for them, and re-layouts  1.67 us (4%)
    pallas_call x1, Pallas kernels, on_device(): pl.pallas_call(functools.partial(kernel, columns), out_shape=jax.ShapeDty...  45.1 us
    unnamed x1, local copies, waits for them, and re-layouts  1.67 us

profile of v1, /device:TPU:96, one launch (start us, length us, event | category | flops | bytes accessed | tf_op | source)
XLA Modules:
  0.0 46.8 jit_solution(15136841968684869390)
XLA Ops:
  0.0 45.1 %shard_map.64 = f32[64,8,128]{2,1,0:T(8,128)} custom-call(f32[64,8,128]{2,1,0:T(8,128)} %field_hbm.1, f32[64,8,128]{2,1,0:T(8,128)} %plane_hbm.1, f32[64,8,128]{2,1,0:T(8,128)} %line_hbm.1, f32[64,8,128]{2,1,0:T(8,128)} %source_hbm.1, f32[8]{0:T(128)} %table_hbm.1, s32[4]{0:T(128)} %index_hbm.1), custom_call_target="tpu_custom_call" | custom-call | tf_op jit(solution)/shard_map/pallas_call | solution.py:336
  45.1 1.7 %copy.8 = f32[64,8,128]{2,1,0:T(8,128)} copy(f32[64,8,128]{2,1,0:T(8,128)} %shard_map.64) | data formatting | bytes 524288

commit v2 on v1

--- a/solution.py
+++ b/solution.py
@@ -9,7 +9,7 @@
 HALF = 4
 ROWS = 8
 LANES = 128
-UNROLL = 4
+UNROLL = 16
 FIELD, PLANE, LINE, SOURCE = range(4)
 MESH = pl.DeviceIdType.MESH
 
@@ -18,11 +18,11 @@
     columns,
     field_hbm, plane_hbm, line_hbm, source_hbm, table_hbm, index_hbm,
     out_hbm,
-    table, index, block, theta, weight, inverse, state, packed, halo,
-    pivots, pivots_in, mixed, planes, planes_in, result,
+    table, index, raw, block, theta, weight, inverse, state, packed, halo,
+    pivots, pivots_in, edge, edge_in, mixed, planes, planes_in, result,
     local_sem, scalar_sem, out_sem,
     swap_send, swap_recv, far_send, far_recv, pass_send, pass_recv,
-    pivot_send, pivot_recv, plane_send, plane_recv,
+    pivot_send, pivot_recv, edge_send, edge_recv, plane_send, plane_recv,
 ):
     layers = field_hbm.shape[0]
     gz, gx, gy = lax.axis_index("gz"), lax.axis_index("gx"), lax.axis_index("gy")
@@ -36,7 +36,7 @@
         return gz * (layers - 1) + (1 - 2 * gz) * k
 
     loads = [
-        pltpu.make_async_copy(source, block.at[a, gx], local_sem.at[a])
+        pltpu.make_async_copy(source, raw.at[a], local_sem.at[a])
         for a, source in enumerate((field_hbm, plane_hbm, line_hbm, source_hbm))
     ]
     scalars = [
@@ -49,6 +49,9 @@
     barrier = pltpu.get_barrier_semaphore()
     pl.semaphore_signal(barrier, inc=1, device_id={"gx": 1 - gx}, device_id_type=MESH)
     pl.semaphore_signal(barrier, inc=1, device_id={"gz": 1 - gz}, device_id_type=MESH)
+    pl.semaphore_signal(
+        barrier, inc=1, device_id={"gz": 1 - gz, "gx": 1 - gx}, device_id_type=MESH
+    )
 
     @pl.when(has_left)
     def _():
@@ -65,6 +68,16 @@
 
     for copy in loads:
         copy.wait()
+
+    def arrange(t, _):
+        for s in range(UNROLL):
+            k = t * UNROLL + s
+            at = layer(k)
+            for a in range(4):
+                block[a, gx, k] = raw[a, at]
+        return 0
+
+    lax.fori_loop(0, layers // UNROLL, arrange, 0)
 
     slots = LANES // 8
     groups = layers // (2 * slots)
@@ -99,7 +112,7 @@
         def steps(t, carry):
             carry = list(carry)
             for s in range(UNROLL):
-                k = layer(t * UNROLL + s)
+                k = t * UNROLL + s
                 line = 1.0 / block[LINE, q, k]
                 for h in range(HALF):
                     th, de = carry[2 * h], carry[2 * h + 1]
@@ -120,7 +133,7 @@
 
     factor(gx)
 
-    signals = 2 + has_left.astype(jnp.int32) + has_right.astype(jnp.int32)
+    signals = 3 + has_left.astype(jnp.int32) + has_right.astype(jnp.int32)
     pl.semaphore_wait(barrier, signals)
 
     def far(side):
@@ -140,6 +153,29 @@
     @pl.when(has_left)
     def _():
         far(1).start()
+
+    def pivot_copy(e):
+        return pltpu.make_async_remote_copy(
+            src_ref=pivots.at[gx],
+            dst_ref=pivots_in.at[gx],
+            send_sem=pivot_send.at[e],
+            recv_sem=pivot_recv.at[e],
+            device_id={"gz": 1 - gz, "gx": lax.rem(gx + e, 2)},
+            device_id_type=MESH,
+        )
+
+    def pivot_arrival(e):
+        return pltpu.make_async_remote_copy(
+            src_ref=pivots.at[gx],
+            dst_ref=pivots_in.at[lax.rem(gx + e, 2)],
+            send_sem=pivot_send.at[e],
+            recv_sem=pivot_recv.at[e],
+            device_id={"gz": 1 - gz, "gx": lax.rem(gx + e, 2)},
+            device_id_type=MESH,
+        )
+
+    for e in range(2):
+        pivot_copy(e).start()
 
     swaps = [
         pltpu.make_async_remote_copy(
@@ -154,21 +190,10 @@
     ]
     for copy in swaps:
         copy.start()
-    for copy in swaps:
+    swaps[0].wait_recv()
+    factor(1 - gx)
+    for copy in swaps[1:]:
         copy.wait_recv()
-    factor(1 - gx)
-
-    def pivot_copy(e):
-        return pltpu.make_async_remote_copy(
-            src_ref=pivots.at[pl.ds(2 * e, 2)],
-            dst_ref=pivots_in.at[pl.ds(2 * e, 2)],
-            send_sem=pivot_send.at[e],
-            recv_sem=pivot_recv.at[e],
-            device_id={"gz": 1 - gz},
-            device_id_type=MESH,
-        )
-
-    pivot_copy(0).start()
 
     def passed(side):
         return pltpu.make_async_remote_copy(
@@ -210,17 +235,47 @@
     lax.fori_loop(0, groups, unpack, 0)
     factor(2)
     factor(3)
-    pivot_copy(1).start()
-    pivot_copy(0).wait_recv()
-    pivot_copy(1).wait_recv()
-    for q in range(4):
+    window = lax.rem(lane + 4, LANES) // 8
+
+    def edge_copy():
+        return pltpu.make_async_remote_copy(
+            src_ref=edge,
+            dst_ref=edge_in,
+            send_sem=edge_send,
+            recv_sem=edge_recv,
+            device_id={"gz": 1 - gz},
+            device_id_type=MESH,
+        )
+
+    slot = 0
+    gathered = zero
+    for q in (2, 3):
         for h in range(HALF):
-            last, step = pivots[q, h, 0], pivots[q, h, 1]
-            other_last, other_step = pivots_in[q, h, 0], pivots_in[q, h, 1]
-            before = last - step
-            share = 1.0 / (before * other_step + step * other_last)
-            mixed[q, h, 0] = other_last * share / before
-            mixed[q, h, 1] = share
+            for c in range(2):
+                moved = pivots[q, h, c]
+                if slot:
+                    moved = pltpu.roll(moved, 8 * slot, 1)
+                gathered = jnp.where(window == slot, moved, gathered)
+                slot += 1
+    edge[...] = gathered
+    edge_copy().start()
+
+    def mix(q, h, other_last, other_step):
+        last, step = pivots[q, h, 0], pivots[q, h, 1]
+        before = last - step
+        share = 1.0 / (before * other_step + step * other_last)
+        ratio = other_last * share / before
+        if q >= 2:
+            share = jnp.where(window == 0, share, 0.0)
+            ratio = jnp.where(window == 0, ratio, 0.0)
+        mixed[q, h, 0] = ratio
+        mixed[q, h, 1] = share
+
+    for e in range(2):
+        pivot_arrival(e).wait_recv()
+    for q in range(2):
+        for h in range(HALF):
+            mix(q, h, pivots_in[q, h, 0], pivots_in[q, h, 1])
 
     first, final = lane == 0, lane == LANES - 1
     top, bottom = row == 0, row == ROWS - 1
@@ -257,7 +312,7 @@
         def forward(t, total, h=h, shift=shift, ends=ends):
             total = list(total)
             for s in range(UNROLL):
-                k = layer(t * UNROLL + s)
+                k = t * UNROLL + s
                 if h == 0:
                     u = [block[FIELD, q, k] for q in range(4)]
                 else:
@@ -271,14 +326,15 @@
             return tuple(total)
 
         total = lax.fori_loop(0, layers // UNROLL, forward, (zero,) * 4)
-        for q in range(4):
+        for q in range(2):
             planes[h, q] = total[q]
+        planes[h, 2] = jnp.where(window == 0, total[2], pltpu.roll(total[3], LANES // 2, 1))
         plane_copy(h).start()
 
         def backward(t, later, h=h):
             later = list(later)
             for s in range(UNROLL):
-                k = layer(layers - 1 - (t * UNROLL + s))
+                k = layers - 1 - (t * UNROLL + s)
                 for q in range(4):
                     here = state[q, k]
                     if s == 0:
@@ -288,17 +344,28 @@
             return tuple(later)
 
         lax.fori_loop(0, layers // UNROLL, backward, (zero,) * 4)
+        if h == 0:
+            edge_copy().wait_recv()
+            arrived = edge_in[...]
+            for q in (2, 3):
+                for i in range(HALF):
+                    slot = ((q - 2) * HALF + i) * 2
+                    pair = [
+                        pltpu.roll(arrived, (LANES - 8 * c) % LANES, 1) if c else arrived
+                        for c in (slot, slot + 1)
+                    ]
+                    mix(q, i, jnp.where(window == 0, pair[0], 1.0), jnp.where(window == 0, pair[1], 1.0))
         plane_copy(h).wait_recv()
-        ends = [
-            mixed[q, h, 0] * planes[h, q] + mixed[q, h, 1] * planes_in[h, q] for q in range(4)
-        ]
+        there = [planes_in[h, q] for q in range(3)]
+        there.append(pltpu.roll(there[2], LANES // 2, 1))
+        ends = [mixed[q, h, 0] * total[q] + mixed[q, h, 1] * there[q] for q in range(4)]
 
     own_end = jnp.where(gx == 0, ends[0], ends[1])
 
     def finish(t, _):
         for s in range(UNROLL):
             k = t * UNROLL + s
-            result[k] = theta[HALF - 1, gx, k] * (state[gx, k] + own_end)
+            result[layer(k)] = theta[HALF - 1, gx, k] * (state[gx, k] + own_end)
         return 0
 
     lax.fori_loop(0, layers // UNROLL, finish, 0)
@@ -322,6 +389,7 @@
 
     for e in range(2):
         pivot_copy(e).wait_send()
+    edge_copy().wait_send()
     for h in range(HALF):
         plane_copy(h).wait_send()
     store.wait()
@@ -341,6 +409,7 @@
         scratch_shapes=[
             pltpu.SMEM(table.shape, f32),
             pltpu.SMEM(index.shape, jnp.int32),
+            pltpu.VMEM((4, layers, *tile), f32),
             pltpu.VMEM((4, 4, layers, *tile), f32),
             pltpu.VMEM((HALF, 4, layers, *tile), f32),
             pltpu.VMEM((HALF, 4, layers, *tile), f32),
@@ -349,14 +418,16 @@
             pltpu.VMEM((2, 4 * groups, *tile), f32),
             pltpu.VMEM((2, 2, 4 * groups, *tile), f32),
             pltpu.VMEM((4, HALF, 2, *tile), f32),
+            pltpu.VMEM((2, HALF, 2, *tile), f32),
+            pltpu.VMEM(tile, f32),
+            pltpu.VMEM(tile, f32),
             pltpu.VMEM((4, HALF, 2, *tile), f32),
-            pltpu.VMEM((4, HALF, 2, *tile), f32),
-            pltpu.VMEM((HALF, 4, *tile), f32),
-            pltpu.VMEM((HALF, 4, *tile), f32),
+            pltpu.VMEM((HALF, 3, *tile), f32),
+            pltpu.VMEM((HALF, 3, *tile), f32),
             pltpu.VMEM((layers, *tile), f32),
             dma((4,)), dma((2,)), dma,
             dma((4,)), dma((4,)), dma((2,)), dma((2,)), dma((2,)), dma((2,)),
-            dma((2,)), dma((2,)), dma((HALF,)), dma((HALF,)),
+            dma((2,)), dma((2,)), dma, dma, dma((HALF,)), dma((HALF,)),
         ],
         compiler_params=pltpu.CompilerParams(
             collective_id=0, has_side_effects=True, vmem_limit_bytes=67043328

time: 47 us -> 28.9 us (0.61)
  Pallas kernels: 45.1 us -> 27 us
    pallas_call x1, Pallas kernels: 45.1 us -> 27 us  [on_device(): pl.pallas_call(functools.partial(kernel, columns), out_shape=jax.ShapeDty...]
where the time goes in v2:
time: 28.9 us; the launch traced here: 28.7 us
  Pallas kernels  27 us (93%)
  local copies, waits for them, and re-layouts  1.67 us (6%)
    pallas_call x1, Pallas kernels, on_device(): pl.pallas_call(functools.partial(kernel, columns), out_shape=jax.ShapeDty...  27 us
    unnamed x1, local copies, waits for them, and re-layouts  1.67 us

profile of v2, /device:TPU:96, one launch (start us, length us, event | category | flops | bytes accessed | tf_op | source)
XLA Modules:
  0.0 28.7 jit_solution(9967634837449092170)
XLA Ops:
  0.0 27.0 %shard_map.64 = f32[64,8,128]{2,1,0:T(8,128)} custom-call(f32[64,8,128]{2,1,0:T(8,128)} %field_hbm.1, f32[64,8,128]{2,1,0:T(8,128)} %plane_hbm.1, f32[64,8,128]{2,1,0:T(8,128)} %line_hbm.1, f32[64,8,128]{2,1,0:T(8,128)} %source_hbm.1, f32[8]{0:T(128)} %table_hbm.1, s32[4]{0:T(128)} %index_hbm.1), custom_call_target="tpu_custom_call" | custom-call | tf_op jit(solution)/shard_map/pallas_call | solution.py:404
  27.0 1.7 %copy.8 = f32[64,8,128]{2,1,0:T(8,128)} copy(f32[64,8,128]{2,1,0:T(8,128)} %shard_map.64) | data formatting | bytes 524288

commit v3 on v1

v3 whole, which is shorter than its diff:
```python
import functools
import jax
import jax.numpy as jnp
from jax import lax
from jax.experimental import pallas as pl
from jax.experimental.pallas import tpu as pltpu
from jax.sharding import PartitionSpec as P

HALF = 4
ROWS = 8
LANES = 128
UNROLL = 16
FIELD, PLANE, LINE, SOURCE = range(4)
MESH = pl.DeviceIdType.MESH


def kernel(
    columns,
    field_hbm, plane_hbm, line_hbm, source_hbm, table_hbm, index_hbm,
    out_hbm,
    table, index, raw, block, theta, weight, inverse, state, packed, halo, halo_beside,
    row_out, row_in, theta_out, theta_in,
    pivots, pivots_in, edge, edge_in, mixed, planes, planes_in, result,
    local_sem, scalar_sem, out_sem,
    far_send, far_recv, beside_send, beside_recv, row_send, row_recv, theta_send, theta_recv,
    pivot_send, pivot_recv, edge_send, edge_recv, plane_send, plane_recv,
):
    layers = field_hbm.shape[0]
    gz, gx, gy = lax.axis_index("gz"), lax.axis_index("gx"), lax.axis_index("gy")
    has_left, has_right = gy > 0, gy < columns - 1
    lane = lax.broadcasted_iota(jnp.int32, (ROWS, LANES), 1)
    row = lax.broadcasted_iota(jnp.int32, (ROWS, LANES), 0)
    zero = jnp.zeros((ROWS, LANES), jnp.float32)
    one = jnp.ones((ROWS, LANES), jnp.float32)
    upper = jnp.full((ROWS, LANES), gx, jnp.int32) == 0

    def layer(k):
        return gz * (layers - 1) + (1 - 2 * gz) * k

    peers = (
        {"gx": 1 - gx},
        {"gz": 1 - gz},
        {"gz": 1 - gz, "gx": 1 - gx},
    )

    def facing(tile):
        return jnp.where(upper, pltpu.roll(tile, 1, 0), tile)

    def beyond(tile):
        first = jnp.broadcast_to(tile[0:1], (ROWS, LANES))
        last = jnp.broadcast_to(tile[ROWS - 1 : ROWS], (ROWS, LANES))
        return jnp.where(upper, first, last)

    loads = [
        pltpu.make_async_copy(source, raw.at[a], local_sem.at[a])
        for a, source in enumerate((field_hbm, plane_hbm, line_hbm, source_hbm))
    ]
    scalars = [
        pltpu.make_async_copy(table_hbm, table, scalar_sem.at[0]),
        pltpu.make_async_copy(index_hbm, index, scalar_sem.at[1]),
    ]
    for copy in scalars + loads:
        copy.start()

    barrier = pltpu.get_barrier_semaphore()
    for peer in peers:
        pl.semaphore_signal(barrier, inc=1, device_id=peer, device_id_type=MESH)

    @pl.when(has_left)
    def _():
        pl.semaphore_signal(barrier, inc=1, device_id={"gy": gy - 1}, device_id_type=MESH)
        pl.semaphore_signal(
            barrier, inc=1, device_id={"gy": gy - 1, "gx": 1 - gx}, device_id_type=MESH
        )

    @pl.when(has_right)
    def _():
        pl.semaphore_signal(barrier, inc=1, device_id={"gy": gy + 1}, device_id_type=MESH)
        pl.semaphore_signal(
            barrier, inc=1, device_id={"gy": gy + 1, "gx": 1 - gx}, device_id_type=MESH
        )

    for copy in scalars:
        copy.wait()
    shifts = [jnp.full((ROWS, LANES), table[index[h]], jnp.float32) for h in range(HALF)]
    inverses = [1.0 / s for s in shifts]

    for copy in loads:
        copy.wait()

    def arrange(t, _):
        for s in range(UNROLL):
            k = t * UNROLL + s
            at = layer(k)
            for a in range(4):
                block[a, 0, k] = raw[a, at]
            row_out[0, 0, pl.ds(k, 1)] = facing(raw[FIELD, at])[0:1]
        return 0

    lax.fori_loop(0, layers // UNROLL, arrange, 0)

    slots = LANES // 8
    groups = layers // (2 * slots)

    def pack(j, _):
        for a in range(4):
            left, right = zero, zero
            for b in range(2):
                for i in range(slots):
                    p = 8 * i + 4 * b
                    moved = block[a, 0, j * 2 * slots + b * slots + i]
                    if p:
                        moved = pltpu.roll(moved, p, 1)
                    at = lane // 4
                    right = jnp.where(at == p // 4, moved, right)
                    left = jnp.where(at == (p // 4 - 1) % 32, moved, left)
            packed[0, a * groups + j] = left
            packed[1, a * groups + j] = right
        return 0

    lax.fori_loop(0, groups, pack, 0)

    for side, missing in ((0, jnp.logical_not(has_left)), (1, jnp.logical_not(has_right))):
        @pl.when(missing)
        def _(side=side):
            for a in range(4):
                for j in range(groups):
                    halo[side, a * groups + j] = one * 1000.0 if a == LINE else zero
            for j in range(groups):
                halo_beside[side, j] = zero

    def factor(q):
        def steps(t, carry):
            carry = list(carry)
            for s in range(UNROLL):
                k = t * UNROLL + s
                line = 1.0 / block[LINE, q, k]
                for h in range(HALF):
                    th, de = carry[2 * h], carry[2 * h + 1]
                    ratio = line * inverses[h]
                    w = ratio * th
                    de = de + w
                    new = th + de
                    theta[h, q, k] = th
                    weight[h, q, k] = w
                    inverse[h, q, k] = 1.0 / (new * th)
                    if h < HALF - 1:
                        theta_out[q, h, pl.ds(k, 1)] = facing(th)[0:1]
                    carry[2 * h], carry[2 * h + 1] = new, de
            return tuple(carry)

        end = lax.fori_loop(0, layers // UNROLL, steps, (one,) * (2 * HALF))
        for h in range(HALF):
            pivots[q, h, 0] = end[2 * h]
            pivots[q, h, 1] = end[2 * h + 1]

    factor(0)

    signals = 3 + 2 * has_left.astype(jnp.int32) + 2 * has_right.astype(jnp.int32)
    pl.semaphore_wait(barrier, signals)

    def far(side):
        return pltpu.make_async_remote_copy(
            src_ref=packed.at[side],
            dst_ref=halo.at[side],
            send_sem=far_send.at[side],
            recv_sem=far_recv.at[side],
            device_id={"gy": gy + 1 - 2 * side},
            device_id_type=MESH,
        )

    def far_beside(side):
        return pltpu.make_async_remote_copy(
            src_ref=packed.at[side, pl.ds(FIELD * groups, groups)],
            dst_ref=halo_beside.at[side],
            send_sem=beside_send.at[side],
            recv_sem=beside_recv.at[side],
            device_id={"gy": gy + 1 - 2 * side, "gx": 1 - gx},
            device_id_type=MESH,
        )

    for side, there in ((0, has_right), (1, has_left)):
        @pl.when(there)
        def _(side=side):
            far(side).start()
            far_beside(side).start()

    def to_peer(source, target, send, recv, e):
        return pltpu.make_async_remote_copy(
            src_ref=source,
            dst_ref=target,
            send_sem=send,
            recv_sem=recv,
            device_id=peers[e],
            device_id_type=MESH,
        )

    def pivot_copy(e):
        return to_peer(pivots.at[0], pivots_in.at[e], pivot_send.at[e], pivot_recv.at[e], e)

    def edge_copy(e):
        return to_peer(edge, edge_in.at[e], edge_send.at[e], edge_recv.at[e], e)

    def plane_copy(h, e):
        return to_peer(
            planes.at[h], planes_in.at[h, e], plane_send.at[h, e], plane_recv.at[h, e], e
        )

    def theta_copy(q):
        return to_peer(theta_out.at[q], theta_in.at[q], theta_send.at[q], theta_recv.at[q], 0)

    def row_copy(h):
        return to_peer(row_out.at[h], row_in.at[h], row_send.at[h], row_recv.at[h], 0)

    first_rows = to_peer(row_out.at[0, 0], row_in.at[0, 0], row_send.at[0], row_recv.at[0], 0)

    first_rows.start()
    for e in range(3):
        pivot_copy(e).start()
    theta_copy(0).start()

    for side, there in ((0, has_left), (1, has_right)):
        @pl.when(there)
        def _(side=side):
            far(side).wait_recv()
            far_beside(side).wait_recv()

    odd = lax.rem(lane // 4, 2) == 1

    def unpack(j, _):
        for a in range(4):
            left, right = halo[0, a * groups + j], halo[1, a * groups + j]
            for b in range(2):
                both = jnp.where(odd, right, left) if b else jnp.where(odd, left, right)
                for i in range(slots):
                    p = 8 * i + 4 * b
                    block[a, 1, j * 2 * slots + b * slots + i] = (
                        pltpu.roll(both, LANES - p, 1) if p else both
                    )
        left, right = halo_beside[0, j], halo_beside[1, j]
        for b in range(2):
            both = jnp.where(odd, right, left) if b else jnp.where(odd, left, right)
            both = jnp.where(upper, both, pltpu.roll(both, 1, 0))
            for i in range(slots):
                p = 8 * i + 4 * b
                moved = pltpu.roll(both, LANES - p, 1) if p else both
                row_in[0, 1, pl.ds(j * 2 * slots + b * slots + i, 1)] = moved[0:1]
        return 0

    lax.fori_loop(0, groups, unpack, 0)
    factor(1)
    theta_copy(1).start()
    window = lax.rem(lane + 4, LANES) // 8
    slot = 0
    gathered = zero
    for h in range(HALF):
        for c in range(2):
            moved = pivots[1, h, c]
            if slot:
                moved = pltpu.roll(moved, 8 * slot, 1)
            gathered = jnp.where(window == slot, moved, gathered)
            slot += 1
    edge[...] = gathered
    for e in range(3):
        edge_copy(e).start()

    def mix(q, h, last, step, other_last, other_step, at):
        before = last - step
        share = 1.0 / (before * other_step + step * other_last)
        ratio = other_last * share / before
        if q:
            share = jnp.where(window == 0, share, 0.0)
            ratio = jnp.where(window == 0, ratio, 0.0)
        mixed[at, q, h, 0] = ratio
        mixed[at, q, h, 1] = share

    for e in range(3):
        pivot_copy(e).wait_recv()
    for h in range(HALF):
        mix(0, h, pivots[0, h, 0], pivots[0, h, 1], pivots_in[1, h, 0], pivots_in[1, h, 1], 0)
        if h < HALF - 1:
            mix(0, h, pivots_in[0, h, 0], pivots_in[0, h, 1], pivots_in[2, h, 0], pivots_in[2, h, 1], 1)

    first, final = lane == 0, lane == LANES - 1
    top, bottom = row == 0, row == ROWS - 1
    join_top = jnp.logical_and(top, jnp.logical_not(upper))
    join_bottom = jnp.logical_and(bottom, upper)
    join = jnp.logical_or(join_top, join_bottom)
    keep_up = jnp.where(top, zero, one)
    keep_down = jnp.where(bottom, zero, one)

    def spread(u, outside):
        lefts = [pltpu.roll(x, 1, 1) for x in u]
        rights = [pltpu.roll(x, LANES - 1, 1) for x in u]
        sums = []
        for q in range(2):
            up = keep_up * pltpu.roll(u[q], 1, 0)
            down = keep_down * pltpu.roll(u[q], ROWS - 1, 0)
            over = jnp.where(join, outside[q], zero)
            left = jnp.where(first, lefts[1 - q], lefts[q])
            right = jnp.where(final, rights[1 - q], rights[q])
            sums.append(((up + down) + over) + (left + right))
        return sums

    first_rows.wait_recv()
    ends = [zero] * 2
    ends_beyond = [zero] * 2
    for h in range(HALF):
        shift = shifts[h]
        if h == 1:
            for q in range(2):
                theta_copy(q).wait_recv()

        def forward(t, total, h=h, shift=shift, ends=ends, ends_beyond=ends_beyond):
            total = list(total)
            for s in range(UNROLL):
                k = t * UNROLL + s
                outside = [
                    jnp.broadcast_to(row_in[h, q, pl.ds(k, 1)], (ROWS, LANES)) for q in range(2)
                ]
                if h == 0:
                    u = [block[FIELD, q, k] for q in range(2)]
                else:
                    u = [theta[h - 1, q, k] * (state[q, k] + ends[q]) for q in range(2)]
                    outside = [
                        jnp.broadcast_to(theta_in[q, h - 1, pl.ds(k, 1)], (ROWS, LANES))
                        * (outside[q] + ends_beyond[q])
                        for q in range(2)
                    ]
                beside = spread(u, outside)
                for q in range(2):
                    flux = block[PLANE, q, k] * (beside[q] - 4.0 * u[q]) + block[SOURCE, q, k]
                    explicit = u[q] + shift * flux
                    total[q] = total[q] + weight[h, q, k] * explicit
                    state[q, k] = inverse[h, q, k] * total[q]
            return tuple(total)

        total = lax.fori_loop(0, layers // UNROLL, forward, (zero,) * 2)
        for q in range(2):
            planes[h, q] = total[q]
        targets = range(3) if h < HALF - 1 else (1,)
        for e in targets:
            plane_copy(h, e).start()

        def backward(t, later, h=h):
            later = list(later)
            for s in range(UNROLL):
                k = layers - 1 - (t * UNROLL + s)
                for q in range(2):
                    here = state[q, k]
                    if s == 0:
                        here = jnp.where(t == 0, zero, here)
                    later[q] = later[q] + here
                    state[q, k] = later[q]
                    if h < HALF - 1:
                        row_out[h + 1, q, pl.ds(k, 1)] = facing(later[q])[0:1]
            return tuple(later)

        lax.fori_loop(0, layers // UNROLL, backward, (zero,) * 2)
        if h < HALF - 1:
            row_copy(h + 1).start()
        if h == 0:
            for e in range(3):
                edge_copy(e).wait_recv()

            def pair(tile, i):
                both = [
                    pltpu.roll(tile, (LANES - 8 * c) % LANES, 1) if c else tile
                    for c in (2 * i, 2 * i + 1)
                ]
                return [jnp.where(window == 0, x, 1.0) for x in both]

            for i in range(HALF):
                mix(1, i, pivots[1, i, 0], pivots[1, i, 1], *pair(edge_in[1], i), 0)
                if i < HALF - 1:
                    mix(1, i, *pair(edge_in[0], i), *pair(edge_in[2], i), 1)
        for e in targets:
            plane_copy(h, e).wait_recv()
        ends = [
            mixed[0, q, h, 0] * total[q] + mixed[0, q, h, 1] * planes_in[h, 1, q] for q in range(2)
        ]
        if h < HALF - 1:
            ends_beyond = [
                beyond(
                    mixed[1, q, h, 0] * planes_in[h, 0, q] + mixed[1, q, h, 1] * planes_in[h, 2, q]
                )
                for q in range(2)
            ]
            row_copy(h + 1).wait_recv()

    def finish(t, _):
        for s in range(UNROLL):
            k = t * UNROLL + s
            result[layer(k)] = theta[HALF - 1, 0, k] * (state[0, k] + ends[0])
        return 0

    lax.fori_loop(0, layers // UNROLL, finish, 0)
    store = pltpu.make_async_copy(result, out_hbm, out_sem)
    store.start()

    for side, there in ((0, has_right), (1, has_left)):
        @pl.when(there)
        def _(side=side):
            far(side).wait_send()
            far_beside(side).wait_send()

    first_rows.wait_send()
    for e in range(3):
        pivot_copy(e).wait_send()
        edge_copy(e).wait_send()
    for q in range(2):
        theta_copy(q).wait_send()
    for h in range(HALF):
        for e in range(3) if h < HALF - 1 else (1,):
            plane_copy(h, e).wait_send()
        if h:
            row_copy(h).wait_send()
    store.wait()


def on_device(columns, field, plane, line, source, table, index):
    layers = field.shape[0]
    tile = (ROWS, LANES)
    f32 = jnp.float32
    groups = layers // 32
    dma = pltpu.SemaphoreType.DMA
    return pl.pallas_call(
        functools.partial(kernel, columns),
        out_shape=jax.ShapeDtypeStruct(field.shape, f32),
        in_specs=[pl.BlockSpec(memory_space=pltpu.HBM)] * 6,
        out_specs=pl.BlockSpec(memory_space=pltpu.HBM),
        scratch_shapes=[
            pltpu.SMEM(table.shape, f32),
            pltpu.SMEM(index.shape, jnp.int32),
            pltpu.VMEM((4, layers, *tile), f32),
            pltpu.VMEM((4, 2, layers, *tile), f32),
            pltpu.VMEM((HALF, 2, layers, *tile), f32),
            pltpu.VMEM((HALF, 2, layers, *tile), f32),
            pltpu.VMEM((HALF, 2, layers, *tile), f32),
            pltpu.VMEM((2, layers, *tile), f32),
            pltpu.VMEM((2, 4 * groups, *tile), f32),
            pltpu.VMEM((2, 4 * groups, *tile), f32),
            pltpu.VMEM((2, groups, *tile), f32),
            pltpu.VMEM((HALF, 2, layers, LANES), f32),
            pltpu.VMEM((HALF, 2, layers, LANES), f32),
            pltpu.VMEM((2, HALF - 1, layers, LANES), f32),
            pltpu.VMEM((2, HALF - 1, layers, LANES), f32),
            pltpu.VMEM((2, HALF, 2, *tile), f32),
            pltpu.VMEM((3, HALF, 2, *tile), f32),
            pltpu.VMEM(tile, f32),
            pltpu.VMEM((3, *tile), f32),
            pltpu.VMEM((2, 2, HALF, 2, *tile), f32),
            pltpu.VMEM((HALF, 2, *tile), f32),
            pltpu.VMEM((HALF, 3, 2, *tile), f32),
            pltpu.VMEM((layers, *tile), f32),
            dma((4,)), dma((2,)), dma,
            dma((2,)), dma((2,)), dma((2,)), dma((2,)), dma((HALF,)), dma((HALF,)), dma((2,)), dma((2,)),
            dma((3,)), dma((3,)), dma((3,)), dma((3,)), dma((HALF, 3)), dma((HALF, 3)),
        ],
        compiler_params=pltpu.CompilerParams(
            collective_id=0, has_side_effects=True, vmem_limit_bytes=67043328
        ),
    )(field, plane, line, source, table, index)


def solution(mesh):
    spec = P("gz", "gx", "gy")
    return jax.shard_map(
        functools.partial(on_device, mesh.shape["gy"]),
        mesh=mesh,
        in_specs=(spec, spec, spec, spec, P(), P()),
        out_specs=spec,
        check_vma=False,
    )
```

time: 47 us -> 26.8 us (0.57)
  Pallas kernels: 45.1 us -> 24.9 us
    pallas_call x1, Pallas kernels: 45.1 us -> 24.9 us  [on_device(): pl.pallas_call(functools.partial(kernel, columns), out_shape=jax.ShapeDty...]
where the time goes in v3:
time: 26.8 us; the launch traced here: 26.6 us
  Pallas kernels  24.9 us (93%)
  local copies, waits for them, and re-layouts  1.67 us (6%)
    pallas_call x1, Pallas kernels, on_device(): pl.pallas_call(functools.partial(kernel, columns), out_shape=jax.ShapeDty...  24.9 us
    unnamed x1, local copies, waits for them, and re-layouts  1.67 us

profile of v3, /device:TPU:96, one launch (start us, length us, event | category | flops | bytes accessed | tf_op | source)
XLA Modules:
  0.0 26.6 jit_solution(12884433844906562452)
XLA Ops:
  0.0 24.9 %shard_map.64 = f32[64,8,128]{2,1,0:T(8,128)} custom-call(f32[64,8,128]{2,1,0:T(8,128)} %field_hbm.1, f32[64,8,128]{2,1,0:T(8,128)} %plane_hbm.1, f32[64,8,128]{2,1,0:T(8,128)} %line_hbm.1, f32[64,8,128]{2,1,0:T(8,128)} %source_hbm.1, f32[8]{0:T(128)} %table_hbm.1, s32[4]{0:T(128)} %index_hbm.1), custom_call_target="tpu_custom_call" | custom-call | tf_op jit(solution)/shard_map/pallas_call | solution.py:427
  24.9 1.7 %copy.8 = f32[64,8,128]{2,1,0:T(8,128)} copy(f32[64,8,128]{2,1,0:T(8,128)} %shard_map.64) | data formatting | bytes 524288

commit v4 on v3

--- a/solution.py
+++ b/solution.py
@@ -313,8 +313,8 @@
 
         def forward(t, total, h=h, shift=shift, ends=ends, ends_beyond=ends_beyond):
             total = list(total)
-            for s in range(UNROLL):
-                k = t * UNROLL + s
+            for s in range(64):
+                k = t * 64 + s
                 outside = [
                     jnp.broadcast_to(row_in[h, q, pl.ds(k, 1)], (ROWS, LANES)) for q in range(2)
                 ]
@@ -335,7 +335,7 @@
                     state[q, k] = inverse[h, q, k] * total[q]
             return tuple(total)
 
-        total = lax.fori_loop(0, layers // UNROLL, forward, (zero,) * 2)
+        total = lax.fori_loop(0, 1, forward, (zero,) * 2)
         for q in range(2):
             planes[h, q] = total[q]
         targets = range(3) if h < HALF - 1 else (1,)

time: 26.8 us -> 26.1 us (0.974)
  Pallas kernels: 24.9 us -> 24.2 us
    pallas_call x1, Pallas kernels: 24.9 us -> 24.2 us  [on_device(): pl.pallas_call(functools.partial(kernel, columns), out_shape=jax.ShapeDty...]
where the time goes in v4:
time: 26.1 us; the launch traced here: 25.9 us
  Pallas kernels  24.2 us (93%)
  local copies, waits for them, and re-layouts  1.67 us (6%)
    pallas_call x1, Pallas kernels, on_device(): pl.pallas_call(functools.partial(kernel, columns), out_shape=jax.ShapeDty...  24.2 us
    unnamed x1, local copies, waits for them, and re-layouts  1.67 us

profile of v4, /device:TPU:96, one launch (start us, length us, event | category | flops | bytes accessed | tf_op | source)
XLA Modules:
  0.0 25.9 jit_solution(3296978052253126661)
XLA Ops:
  0.0 24.2 %shard_map.64 = f32[64,8,128]{2,1,0:T(8,128)} custom-call(f32[64,8,128]{2,1,0:T(8,128)} %field_hbm.1, f32[64,8,128]{2,1,0:T(8,128)} %plane_hbm.1, f32[64,8,128]{2,1,0:T(8,128)} %line_hbm.1, f32[64,8,128]{2,1,0:T(8,128)} %source_hbm.1, f32[8]{0:T(128)} %table_hbm.1, s32[4]{0:T(128)} %index_hbm.1), custom_call_target="tpu_custom_call" | custom-call | tf_op jit(solution)/shard_map/pallas_call | solution.py:427
  24.2 1.7 %copy.8 = f32[64,8,128]{2,1,0:T(8,128)} copy(f32[64,8,128]{2,1,0:T(8,128)} %shard_map.64) | data formatting | bytes 524288

commit v5 on v1

v5 whole, which is shorter than its diff:
```python
import functools
import jax
import jax.numpy as jnp
from jax import lax
from jax.experimental import pallas as pl
from jax.experimental.pallas import tpu as pltpu
from jax.sharding import PartitionSpec as P

HALF = 4
ROWS = 8
LANES = 128
UNROLL = 16
SPAN = 64
FIELD, PLANE, LINE, SOURCE = range(4)
MESH = pl.DeviceIdType.MESH


def turn(tile, shift):
    shift %= LANES
    return pltpu.roll(tile, shift, 1) if shift else tile


def kernel(
    columns,
    field_hbm, plane_hbm, line_hbm, source_hbm, table_hbm, index_hbm,
    out_hbm,
    table, index, raw, block, swapped, theta, weight, inverse, state,
    far_out, far_in, near_out, near_in, far_turned, near_turned, far_merged, near_merged, strip_out, strip_in, strip_end,
    row_out, row_in, theta_out, theta_in,
    pivots, pivots_in, mixed, planes, planes_in, result,
    local_sem, scalar_sem, out_sem,
    far_send, far_recv, near_send, near_recv, swap_send, swap_recv, strip_send, strip_recv,
    row_send, row_recv, theta_send, theta_recv, pivot_send, pivot_recv, plane_send, plane_recv,
):
    layers = field_hbm.shape[0]
    gz, gx, gy = lax.axis_index("gz"), lax.axis_index("gx"), lax.axis_index("gy")
    has_left, has_right = gy > 0, gy < columns - 1
    solver = gx == 1
    wants_left = jnp.logical_and(solver, jnp.logical_and(gz == 0, has_left))
    wants_right = jnp.logical_and(solver, jnp.logical_and(gz == 1, has_right))
    lacks = jnp.logical_and(
        solver, jnp.logical_not(jnp.logical_or(wants_left, wants_right))
    )
    lane = lax.broadcasted_iota(jnp.int32, (ROWS, LANES), 1)
    row = lax.broadcasted_iota(jnp.int32, (ROWS, LANES), 0)
    zero = jnp.zeros((ROWS, LANES), jnp.float32)
    one = jnp.ones((ROWS, LANES), jnp.float32)
    upper = jnp.full((ROWS, LANES), gx, jnp.int32) == 0
    half = LANES // 2

    def part(offset, size):
        return lax.rem(lane - offset + LANES, LANES) // size

    def layer(k):
        return gz * (layers - 1) + (1 - 2 * gz) * k

    peers = (
        {"gx": 1 - gx},
        {"gz": 1 - gz},
        {"gz": 1 - gz, "gx": 1 - gx},
    )

    def facing(tile):
        return jnp.where(upper, pltpu.roll(tile, 1, 0), tile)

    def beyond(tile):
        first = jnp.broadcast_to(tile[0:1], (ROWS, LANES))
        last = jnp.broadcast_to(tile[ROWS - 1 : ROWS], (ROWS, LANES))
        return jnp.where(upper, first, last)

    loads = [
        pltpu.make_async_copy(source, raw.at[a], local_sem.at[a])
        for a, source in enumerate((field_hbm, plane_hbm, line_hbm, source_hbm))
    ]
    scalars = [
        pltpu.make_async_copy(table_hbm, table, scalar_sem.at[0]),
        pltpu.make_async_copy(index_hbm, index, scalar_sem.at[1]),
    ]
    for copy in scalars + loads:
        copy.start()

    barrier = pltpu.get_barrier_semaphore()
    beside = ({}, {"gx": 1 - gx}, {"gz": 1 - gz}, {"gz": 1 - gz, "gx": 1 - gx})
    for step, there in ((-1, has_left), (1, has_right)):
        @pl.when(there)
        def _(step=step):
            for other in beside:
                pl.semaphore_signal(
                    barrier, inc=1, device_id={"gy": gy + step, **other}, device_id_type=MESH
                )

    for peer in peers:
        pl.semaphore_signal(barrier, inc=1, device_id=peer, device_id_type=MESH)

    for copy in scalars:
        copy.wait()
    shifts = [jnp.full((ROWS, LANES), table[index[h]], jnp.float32) for h in range(HALF)]
    inverses = [1.0 / s for s in shifts]

    for copy in loads:
        copy.wait()

    def arrange(t, _):
        for s in range(UNROLL):
            k = t * UNROLL + s
            at = layer(k)
            for a in range(4):
                block[a, 0, k] = raw[a, at]
            row_out[0, pl.ds(k, 1)] = facing(raw[FIELD, at])[0:1]
        return 0

    lax.fori_loop(0, layers // UNROLL, arrange, 0)

    slots = LANES // 8
    groups = layers // (2 * slots)

    def pack(j, _):
        at = lane // 4
        for a in range(4):
            left, right = zero, zero
            for b in range(2):
                near = zero
                near_slot = part(4 * b - 8 + 8 * gz, 8)
                for i in range(slots):
                    p = 8 * i + 4 * b
                    moved = turn(block[a, 0, j * 2 * slots + b * slots + i], p)
                    right = jnp.where(at == p // 4, moved, right)
                    left = jnp.where(at == (p // 4 - 1) % 32, moved, left)
                    near = jnp.where(near_slot == i, moved, near)
                near_out[a * 2 * groups + 2 * j + b] = near
            far_out[0, a * groups + j] = left
            far_out[1, a * groups + j] = right
        return 0

    lax.fori_loop(0, groups, pack, 0)

    @pl.when(lacks)
    def _():
        for q in range(4):
            for a in range(4):
                for j in range(groups):
                    far_in[q, a * groups + j] = one * 1000.0 if a == LINE else zero

    def factor(q):
        def steps(t, carry):
            carry = list(carry)
            for s in range(UNROLL):
                k = t * UNROLL + s
                line = 1.0 / block[LINE, q, k]
                for h in range(HALF):
                    th, de = carry[2 * h], carry[2 * h + 1]
                    ratio = line * inverses[h]
                    w = ratio * th
                    de = de + w
                    new = th + de
                    theta[h, q, k] = th
                    weight[h, q, k] = w
                    inverse[h, q, k] = 1.0 / (new * th)
                    if q == 0 and h < HALF - 1:
                        theta_out[h, pl.ds(k, 1)] = facing(th)[0:1]
                    carry[2 * h], carry[2 * h + 1] = new, de
            return tuple(carry)

        return lax.fori_loop(0, layers // UNROLL, steps, (one,) * (2 * HALF))

    @pl.when(solver)
    def _():
        def shift_own(t, _):
            for s in range(UNROLL):
                k = t * UNROLL + s
                for a in range(4):
                    block[a, 1, k] = turn(block[a, 0, k], 32)
            return 0

        lax.fori_loop(0, layers // UNROLL, shift_own, 0)

    found = factor(0)
    for h in range(HALF):
        pivots[h, 0] = found[2 * h]
        pivots[h, 1] = found[2 * h + 1]

    pl.semaphore_wait(barrier, 3 + 4 * has_left.astype(jnp.int32) + 4 * has_right.astype(jnp.int32))

    def send(source, target, send_sem, recv_sem, device):
        return pltpu.make_async_remote_copy(
            src_ref=source,
            dst_ref=target,
            send_sem=send_sem,
            recv_sem=recv_sem,
            device_id=device,
            device_id_type=MESH,
        )

    from_left = 2 * gz + gx
    from_right = 2 * (1 - gz) + gx

    def far(way, quarter):
        device = {"gy": gy + 1 - 2 * way}
        if quarter // 2:
            device["gz"] = 1 - gz
        if quarter % 2 == 0:
            device["gx"] = 1 - gx
        return send(
            far_out.at[way], far_in.at[quarter], far_send.at[way], far_recv.at[quarter], device
        )

    def far_arrival(quarter):
        return send(
            far_out.at[0], far_in.at[quarter], far_send.at[0], far_recv.at[quarter], peers[0]
        )

    def near(x):
        return send(near_out, near_in.at[x], near_send, near_recv.at[x], {"gz": 1 - gz, "gx": 1})

    def near_arrival(x):
        return send(near_out, near_in.at[x], near_send, near_recv.at[x], peers[1])

    def swap(a):
        return send(
            block.at[a, 0], swapped.at[a], swap_send.at[a], swap_recv.at[a], {"gx": 1 - gx}
        )

    def pivot_copy(e):
        return send(pivots, pivots_in.at[e], pivot_send.at[e], pivot_recv.at[e], peers[e])

    def plane_copy(h, e):
        return send(
            planes.at[h], planes_in.at[h, e], plane_send.at[h, e], plane_recv.at[h, e], peers[e]
        )

    def row_copy(h):
        rows = pl.ds(0, layers)
        return send(
            row_out.at[h, rows], row_in.at[h, rows], row_send.at[h], row_recv.at[h], peers[0]
        )

    every = (pl.ds(0, HALF - 1), pl.ds(0, layers))
    theta_copy = send(theta_out.at[every], theta_in.at[every], theta_send, theta_recv, peers[0])

    def strip_copy(e, side):
        return send(
            strip_out, strip_in.at[side], strip_send.at[e], strip_recv.at[side], peers[e]
        )

    def strip_arrival(side):
        return send(
            strip_out, strip_in.at[side], strip_send.at[0], strip_recv.at[side], peers[0]
        )

    row_copy(0).start()
    for way, there, place in ((0, has_right, from_left), (1, has_left, from_right)):
        @pl.when(there)
        def _(way=way, place=place):
            for quarter in range(4):
                @pl.when(place == quarter)
                def _(quarter=quarter):
                    far(way, quarter).start()

    for e in range(3):
        pivot_copy(e).start()
    for x in range(2):
        @pl.when(gx == x)
        def _(x=x):
            near(x).start()

    theta_copy.start()

    @pl.when(gx == 0)
    def _():
        for a in range(4):
            swap(a).start()

    top, bottom = row == 0, row == ROWS - 1
    join = jnp.logical_or(
        jnp.logical_and(top, jnp.logical_not(upper)), jnp.logical_and(bottom, upper)
    )
    keep_up = jnp.where(top, zero, one)
    keep_down = jnp.where(bottom, zero, one)
    keep_left = jnp.where(lane == 0, zero, one)
    keep_right = jnp.where(lane == LANES - 1, zero, one)

    def spread(u, outside):
        up = keep_up * pltpu.roll(u, 1, 0)
        down = keep_down * pltpu.roll(u, ROWS - 1, 0)
        over = jnp.where(join, outside, zero)
        left = keep_left * turn(u, 1)
        right = keep_right * turn(u, -1)
        return ((up + down) + over) + (left + right)

    region = part(-8, 32)
    lower_rows = lax.rem(region, 2) == 1
    cross_up = jnp.logical_and(top, lower_rows)
    cross_down = jnp.logical_and(bottom, jnp.logical_not(lower_rows))

    def strip_spread(u):
        above, below = pltpu.roll(u, 1, 0), pltpu.roll(u, ROWS - 1, 0)
        up = jnp.where(cross_up, turn(above, 32), keep_up * above)
        down = jnp.where(cross_down, turn(below, -32), keep_down * below)
        return (up + down) + (turn(u, 1) + turn(u, -1))

    def eliminate(h, q, values):
        shift = shifts[h]

        def forward(t, total):
            for s in range(SPAN):
                k = t * SPAN + s
                u, beside = values(k)
                flux = block[PLANE, q, k] * (beside - 4.0 * u) + block[SOURCE, q, k]
                total = total + weight[h, q, k] * (u + shift * flux)
                state[q, k] = inverse[h, q, k] * total
            return total

        return lax.fori_loop(0, layers // SPAN, forward, zero)

    def substitute(h, q):
        def backward(t, later):
            for s in range(UNROLL):
                k = layers - 1 - (t * UNROLL + s)
                here = state[q, k]
                if s == 0:
                    here = jnp.where(t == 0, zero, here)
                later = later + here
                state[q, k] = later
                if q == 0 and h < HALF - 1:
                    row_out[h + 1, pl.ds(k, 1)] = facing(later)[0:1]
            return later

        lax.fori_loop(0, layers // UNROLL, backward, zero)

    def targets(h):
        return range(3) if h < HALF - 1 else (1,)

    now = {}

    def run(h):
        end, end_beyond = now.get("end"), now.get("beyond")

        def values(k):
            outside = jnp.broadcast_to(row_in[h, pl.ds(k, 1)], (ROWS, LANES))
            if h == 0:
                u = block[FIELD, 0, k]
            else:
                u = theta[h - 1, 0, k] * (state[0, k] + end)
                outside = jnp.broadcast_to(theta_in[h - 1, pl.ds(k, 1)], (ROWS, LANES)) * (
                    outside + end_beyond
                )
            return u, spread(u, outside)

        total = eliminate(h, 0, values)
        now["total"] = total
        planes[h] = total
        for e in targets(h):
            plane_copy(h, e).start()
        substitute(h, 0)
        if h < HALF - 1:
            row_copy(h + 1).start()

    def settle(h):
        for e in targets(h):
            plane_copy(h, e).wait_recv()
        now["end"] = mixed[0, h, 0] * now["total"] + mixed[0, h, 1] * planes_in[h, 1]
        if h < HALF - 1:
            now["beyond"] = beyond(
                mixed[1, h, 0] * planes_in[h, 0] + mixed[1, h, 1] * planes_in[h, 2]
            )
            row_copy(h + 1).wait_recv()

    def mix(at, h, last, step, other_last, other_step):
        before = last - step
        share = 1.0 / (before * other_step + step * other_last)
        mixed[at, h, 0] = other_last * share / before
        mixed[at, h, 1] = share

    def merge(source, turned, merged, count, quarters):
        for d in range(4):
            for q in range(count):
                for at in range(source.shape[1]):
                    turned[d, q, at] = turn(source[q, at], 32 * d)
        for b in range(2):
            pick = quarters(b)
            for a in range(4):
                for j in range(groups):
                    at = a * groups + j
                    if count == 2:
                        at = a * 2 * groups + 2 * j + b
                    for m in range(4):
                        tiles = [turned[(4 - count + q - m) % 4, q, at] for q in range(count)]
                        tile = tiles[-1]
                        for q in range(count - 1):
                            tile = jnp.where(pick == 4 - count + q, tiles[q], tile)
                        merged[b, (a * groups + j) * 4 + m] = tile

    def strip_near():
        for a in range(4):
            swap(a).wait_recv()
        for x in range(2):
            near_arrival(x).wait_recv()
        merge(near_in, near_turned, near_merged, 2, lambda b: part(4 * b - 8 * gz, 32))

    def strip_far():
        @pl.when(jnp.logical_or(wants_left, wants_right))
        def _():
            for q in range(4):
                far_arrival(q).wait_recv()

        merge(far_in, far_turned, far_merged, 4, lambda b: part(4 * b - 4 + 4 * gz, 32))
        outer = lax.rem(lane + 4 - 4 * gz, 32) < 4

        for n in range(8):
            def gather(j, _, n=n):
                for a in range(4):
                    for m in range(4):
                        at = (a * groups + j) * 4 + m
                        k = j * 2 * slots + 4 * m + n % 2 * slots + n // 2
                        there = turn(near_merged[n % 2, at], -4 * n)
                        tile = turn(far_merged[n % 2, at], -4 * n)
                        own = jnp.where(region == 0, swapped[a, k], block[a, 1, k])
                        own = jnp.where(region < 2, own, there)
                        block[a, 1, k] = jnp.where(outer, tile, own)
                return 0

            lax.fori_loop(0, groups, gather, 0)

        ends = factor(1)
        for h in range(HALF):
            last, step = ends[2 * h], ends[2 * h + 1]
            mix(2, h, last, step, turn(last, half), turn(step, half))

    def strip_run(h):
        end = strip_end[...] if h else None

        def values(k):
            u = theta[h - 1, 1, k] * (state[1, k] + end) if h else block[FIELD, 1, k]
            return u, strip_spread(u)

        total = eliminate(h, 1, values)
        substitute(h, 1)
        strip_end[...] = mixed[2, h, 0] * total + mixed[2, h, 1] * turn(total, half)

    def strip_share():
        end = strip_end[...]
        slot = lax.rem(lane + 4 * gz, 32) // 4

        tiles = [zero] * (layers // 8)
        for i in range(8):
            for v in range(layers // 8):
                k = v * 8 + i
                moved = turn(theta[HALF - 1, 1, k] * (state[1, k] + end), 4 * i)
                tiles[v] = jnp.where(slot == i, moved, tiles[v])
        for v in range(layers // 8):
            strip_out[v] = tiles[v]
        for side in range(2):
            @pl.when(gz == side)
            def _(side=side):
                for e in (1, 2, 0):
                    strip_copy(e, side).start()
                for v in range(layers // 8):
                    strip_in[side, v] = tiles[v]

    row_copy(0).wait_recv()
    run(0)
    for e in range(3):
        pivot_copy(e).wait_recv()
    for h in range(HALF):
        mix(0, h, pivots[h, 0], pivots[h, 1], pivots_in[1, h, 0], pivots_in[1, h, 1])
        if h < HALF - 1:
            mix(1, h, pivots_in[0, h, 0], pivots_in[0, h, 1], pivots_in[2, h, 0], pivots_in[2, h, 1])
    settle(0)
    theta_copy.wait_recv()
    run(1)

    @pl.when(solver)
    def _():
        strip_near()
        strip_far()
        strip_run(0)

    settle(1)
    run(2)

    @pl.when(solver)
    def _():
        strip_run(1)
        strip_run(2)
        strip_run(3)
        strip_share()

    settle(2)
    run(3)

    settle(3)
    end = now["end"]

    @pl.when(jnp.logical_or(gx == 0, gz == 1))
    def _():
        strip_arrival(0).wait_recv()

    @pl.when(jnp.logical_or(gx == 0, gz == 0))
    def _():
        strip_arrival(1).wait_recv()

    lower_core = jnp.full((ROWS, LANES), gx, jnp.int32) == 1
    for side in range(2):
        other_half = jnp.full((ROWS, LANES), gz, jnp.int32) != side
        for v in range(layers // 8):
            tile = strip_in[side, v]
            tile = jnp.where(other_half, turn(tile, half), tile)
            strip_in[side, v] = jnp.where(lower_core, turn(tile, -32), tile)

    for i in range(8):
        for v in range(layers // 8):
            k = v * 8 + i
            left = turn(strip_in[0, v], -4 * i)
            right = turn(strip_in[1, v], -4 * i)
            inner = theta[HALF - 1, 0, k] * (state[0, k] + end)
            inner = jnp.where(lane < 4, left, inner)
            result[layer(k)] = jnp.where(lane >= LANES - 4, right, inner)
    store = pltpu.make_async_copy(result, out_hbm, out_sem)
    store.start()

    for way, there in ((0, has_right), (1, has_left)):
        @pl.when(there)
        def _(way=way):
            far(way, 0).wait_send()

    @pl.when(gx == 0)
    def _():
        for a in range(4):
            swap(a).wait_send()

    @pl.when(solver)
    def _():
        for e in range(3):
            strip_copy(e, 0).wait_send()

    near(0).wait_send()
    theta_copy.wait_send()
    for e in range(3):
        pivot_copy(e).wait_send()
    for h in range(HALF):
        row_copy(h).wait_send()
        for e in targets(h):
            plane_copy(h, e).wait_send()
    store.wait()


def on_device(columns, field, plane, line, source, table, index):
    layers = field.shape[0]
    tile = (ROWS, LANES)
    f32 = jnp.float32
    groups = layers // 32
    dma = pltpu.SemaphoreType.DMA
    return pl.pallas_call(
        functools.partial(kernel, columns),
        out_shape=jax.ShapeDtypeStruct(field.shape, f32),
        in_specs=[pl.BlockSpec(memory_space=pltpu.HBM)] * 6,
        out_specs=pl.BlockSpec(memory_space=pltpu.HBM),
        scratch_shapes=[
            pltpu.SMEM(table.shape, f32),
            pltpu.SMEM(index.shape, jnp.int32),
            pltpu.VMEM((4, layers, *tile), f32),
            pltpu.VMEM((4, 2, layers, *tile), f32),
            pltpu.VMEM((4, layers, *tile), f32),
            pltpu.VMEM((HALF, 2, layers, *tile), f32),
            pltpu.VMEM((HALF, 2, layers, *tile), f32),
            pltpu.VMEM((HALF, 2, layers, *tile), f32),
            pltpu.VMEM((2, layers, *tile), f32),
            pltpu.VMEM((2, 4 * groups, *tile), f32),
            pltpu.VMEM((4, 4 * groups, *tile), f32),
            pltpu.VMEM((8 * groups, *tile), f32),
            pltpu.VMEM((2, 8 * groups, *tile), f32),
            pltpu.VMEM((4, 4, 4 * groups, *tile), f32),
            pltpu.VMEM((4, 2, 8 * groups, *tile), f32),
            pltpu.VMEM((2, 16 * groups, *tile), f32),
            pltpu.VMEM((2, 16 * groups, *tile), f32),
            pltpu.VMEM((layers // 8, *tile), f32),
            pltpu.VMEM((2, layers // 8, *tile), f32),
            pltpu.VMEM(tile, f32),
            pltpu.VMEM((HALF, layers + ROWS, LANES), f32),
            pltpu.VMEM((HALF, layers + ROWS, LANES), f32),
            pltpu.VMEM((HALF - 1, layers + ROWS, LANES), f32),
            pltpu.VMEM((HALF - 1, layers + ROWS, LANES), f32),
            pltpu.VMEM((HALF, 2, *tile), f32),
            pltpu.VMEM((3, HALF, 2, *tile), f32),
            pltpu.VMEM((3, HALF, 2, *tile), f32),
            pltpu.VMEM((HALF, *tile), f32),
            pltpu.VMEM((HALF, 3, *tile), f32),
            pltpu.VMEM((layers, *tile), f32),
            dma((4,)), dma((2,)), dma,
            dma((2,)), dma((4,)), dma, dma((2,)), dma((4,)), dma((4,)), dma((3,)), dma((2,)),
            dma((HALF,)), dma((HALF,)), dma, dma, dma((3,)), dma((3,)), dma((HALF, 3)), dma((HALF, 3)),
        ],
        compiler_params=pltpu.CompilerParams(
            collective_id=0, has_side_effects=True, vmem_limit_bytes=67043328
        ),
    )(field, plane, line, source, table, index)


def solution(mesh):
    spec = P("gz", "gx", "gy")
    return jax.shard_map(
        functools.partial(on_device, mesh.shape["gy"]),
        mesh=mesh,
        in_specs=(spec, spec, spec, spec, P(), P()),
        out_specs=spec,
        check_vma=False,
    )
```

time: 47 us -> 23 us (0.49)
  Pallas kernels: 45.1 us -> 21.1 us
    pallas_call x1, Pallas kernels: 45.1 us -> 21.1 us  [on_device(): pl.pallas_call(functools.partial(kernel, columns), out_shape=jax.ShapeDty...]
where the time goes in v5:
time: 23 us; the launch traced here: 22.8 us
  Pallas kernels  21.1 us (92%)
  local copies, waits for them, and re-layouts  1.67 us (7%)
    pallas_call x1, Pallas kernels, on_device(): pl.pallas_call(functools.partial(kernel, columns), out_shape=jax.ShapeDty...  21.1 us
    unnamed x1, local copies, waits for them, and re-layouts  1.67 us

profile of v5, /device:TPU:96, one launch (start us, length us, event | category | flops | bytes accessed | tf_op | source)
XLA Modules:
  0.0 22.8 jit_solution(3326360929962455122)
XLA Ops:
  0.0 21.1 %shard_map.64 = f32[64,8,128]{2,1,0:T(8,128)} custom-call(f32[64,8,128]{2,1,0:T(8,128)} %field_hbm.1, f32[64,8,128]{2,1,0:T(8,128)} %plane_hbm.1, f32[64,8,128]{2,1,0:T(8,128)} %line_hbm.1, f32[64,8,128]{2,1,0:T(8,128)} %source_hbm.1, f32[8]{0:T(128)} %table_hbm.1, s32[4]{0:T(128)} %index_hbm.1), custom_call_target="tpu_custom_call" | custom-call | tf_op jit(solution)/shard_map/pallas_call | solution.py:553
  21.1 1.7 %copy.8 = f32[64,8,128]{2,1,0:T(8,128)} copy(f32[64,8,128]{2,1,0:T(8,128)} %shard_map.64) | data formatting | bytes 524288

commit v6 on v5

--- a/solution.py
+++ b/solution.py
@@ -81,8 +81,8 @@
 
     barrier = pltpu.get_barrier_semaphore()
     beside = ({}, {"gx": 1 - gx}, {"gz": 1 - gz}, {"gz": 1 - gz, "gx": 1 - gx})
-    for step, there in ((-1, has_left), (1, has_right)):
-        @pl.when(there)
+    for step, wanted in ((-1, wants_left), (1, wants_right)):
+        @pl.when(wanted)
         def _(step=step):
             for other in beside:
                 pl.semaphore_signal(
@@ -179,7 +179,7 @@
         pivots[h, 0] = found[2 * h]
         pivots[h, 1] = found[2 * h + 1]
 
-    pl.semaphore_wait(barrier, 3 + 4 * has_left.astype(jnp.int32) + 4 * has_right.astype(jnp.int32))
+    pl.semaphore_wait(barrier, 3 + has_left.astype(jnp.int32) + has_right.astype(jnp.int32))
 
     def send(source, target, send_sem, recv_sem, device):
         return pltpu.make_async_remote_copy(

time: 23 us -> 22.1 us (0.961)
  Pallas kernels: 21.1 us -> 20.3 us
    pallas_call x1, Pallas kernels: 21.1 us -> 20.3 us  [on_device(): pl.pallas_call(functools.partial(kernel, columns), out_shape=jax.ShapeDty...]
where the time goes in v6:
time: 22.1 us; the launch traced here: 22 us
  Pallas kernels  20.3 us (92%)
  local copies, waits for them, and re-layouts  1.67 us (8%)
    pallas_call x1, Pallas kernels, on_device(): pl.pallas_call(functools.partial(kernel, columns), out_shape=jax.ShapeDty...  20.3 us
    unnamed x1, local copies, waits for them, and re-layouts  1.67 us

profile of v6, /device:TPU:96, one launch (start us, length us, event | category | flops | bytes accessed | tf_op | source)
XLA Modules:
  0.0 22.0 jit_solution(16965450223394695536)
XLA Ops:
  0.0 20.3 %shard_map.64 = f32[64,8,128]{2,1,0:T(8,128)} custom-call(f32[64,8,128]{2,1,0:T(8,128)} %field_hbm.1, f32[64,8,128]{2,1,0:T(8,128)} %plane_hbm.1, f32[64,8,128]{2,1,0:T(8,128)} %line_hbm.1, f32[64,8,128]{2,1,0:T(8,128)} %source_hbm.1, f32[8]{0:T(128)} %table_hbm.1, s32[4]{0:T(128)} %index_hbm.1), custom_call_target="tpu_custom_call" | custom-call | tf_op jit(solution)/shard_map/pallas_call | solution.py:553
  20.3 1.7 %copy.8 = f32[64,8,128]{2,1,0:T(8,128)} copy(f32[64,8,128]{2,1,0:T(8,128)} %shard_map.64) | data formatting | bytes 524288

commit v7 on v6

--- a/solution.py
+++ b/solution.py
@@ -114,25 +114,27 @@
     slots = LANES // 8
     groups = layers // (2 * slots)
 
-    def pack(j, _):
-        at = lane // 4
-        for a in range(4):
-            left, right = zero, zero
-            for b in range(2):
-                near = zero
-                near_slot = part(4 * b - 8 + 8 * gz, 8)
-                for i in range(slots):
-                    p = 8 * i + 4 * b
-                    moved = turn(block[a, 0, j * 2 * slots + b * slots + i], p)
-                    right = jnp.where(at == p // 4, moved, right)
-                    left = jnp.where(at == (p // 4 - 1) % 32, moved, left)
-                    near = jnp.where(near_slot == i, moved, near)
-                near_out[a * 2 * groups + 2 * j + b] = near
-            far_out[0, a * groups + j] = left
-            far_out[1, a * groups + j] = right
+    near_slots = [part(4 * b - 8 + 8 * gz, 8) for b in range(2)]
+    quad = lane // 4
+
+    def pack(a, _):
+        left, right = [zero] * groups, [zero] * groups
+        near = [zero] * (2 * groups)
+        for n in range(2 * slots):
+            i, b = n // 2, n % 2
+            for j in range(groups):
+                moved = turn(block[a, 0, j * 2 * slots + b * slots + i], 4 * n)
+                right[j] = jnp.where(quad == n, moved, right[j])
+                left[j] = jnp.where(quad == (n - 1) % 32, moved, left[j])
+                near[2 * j + b] = jnp.where(near_slots[b] == i, moved, near[2 * j + b])
+        for j in range(groups):
+            far_out[0, a * groups + j] = left[j]
+            far_out[1, a * groups + j] = right[j]
+        for j in range(2 * groups):
+            near_out[a * 2 * groups + j] = near[j]
         return 0
 
-    lax.fori_loop(0, groups, pack, 0)
+    lax.fori_loop(0, 4, pack, 0)
 
     @pl.when(lacks)
     def _():

time: 22.1 us -> 22.1 us (level)
  no operation moved by 1% of the time
where the time goes in v7:
time: 22.1 us; the launch traced here: 22 us
  Pallas kernels  20.3 us (92%)
  local copies, waits for them, and re-layouts  1.67 us (8%)
    pallas_call x1, Pallas kernels, on_device(): pl.pallas_call(functools.partial(kernel, columns), out_shape=jax.ShapeDty...  20.3 us
    unnamed x1, local copies, waits for them, and re-layouts  1.67 us

profile of v7, /device:TPU:96, one launch (start us, length us, event | category | flops | bytes accessed | tf_op | source)
XLA Modules:
  0.0 22.0 jit_solution(189219448750890365)
XLA Ops:
  0.0 20.3 %shard_map.64 = f32[64,8,128]{2,1,0:T(8,128)} custom-call(f32[64,8,128]{2,1,0:T(8,128)} %field_hbm.1, f32[64,8,128]{2,1,0:T(8,128)} %plane_hbm.1, f32[64,8,128]{2,1,0:T(8,128)} %line_hbm.1, f32[64,8,128]{2,1,0:T(8,128)} %source_hbm.1, f32[8]{0:T(128)} %table_hbm.1, s32[4]{0:T(128)} %index_hbm.1), custom_call_target="tpu_custom_call" | custom-call | tf_op jit(solution)/shard_map/pallas_call | solution.py:555
  20.3 1.7 %copy.8 = f32[64,8,128]{2,1,0:T(8,128)} copy(f32[64,8,128]{2,1,0:T(8,128)} %shard_map.64) | data formatting | bytes 524288
